TPU v7x, 128 devices: a whole 4x4x4 slice. The times are simulated.
128 devices in a mesh: row: 16 (over x_hi, y, core), col: 8 (over x_lo, z).
Axes of the slice: x: 4 (x_hi: 2, x_lo: 2; x = x_hi * 2 + x_lo), y: 4, z: 4, core: 2. Of those that a mesh axis runs over, the one named last changes fastest.
Arguments:
- object_core: float32 [4, 4096, 2048], P(None, 'row', 'col'), may hold values from -4.2 to 4.2
- probe_field: float32 [2, 256, 256], replicated, may hold values from -4.2 to 4.2
- offsets: int32 [16, 8, 3, 2], P('row', 'col'), may hold values from 0 to 256
- tile_counts: int32 [16, 8], P('row', 'col'), may hold values from 1 to 3, as said below
- intensity: float32 [16, 8, 3, 256, 256], P('row', 'col'), may hold values from 0.25 to 2
Outputs:
- object_next: float32 [4, 4096, 2048], P(None, 'row', 'col')
Inputs may be any that keep to these rules, and one draw needn't show every extreme that they name: offsets of the probe window inside a tile's patch of side 512; slots at or past the tile's count are unused. `tile_counts`: some tile holds 3 positions.
All inputs are finite; a program needn't handle non-finite values.
Results may differ from a plain program's by a relative error of at most 0.0003.
Values sent between devices are 32-bit elements; how exact they have to be, the bound alone decides.
No kernel may reach another device: no remote copies, remote signals or barrier semaphores. Data moves between devices by JAX's collectives and lax.ppermute only.
A program may use at most 128 MiB of HBM per device.

v0:
```python
import functools

import jax
import jax.numpy as jnp
import numpy as np
from jax import lax
from jax.experimental import pallas as pl
from jax.experimental.pallas import tpu as pltpu
from jax.sharding import PartitionSpec as P

PROBE = 256
HALF = 128
SLICES = 2
SLOTS = 3
ITERS = 2
CHANNELS = 2 * SLICES
FRESNEL = 24.0
STEP_SIZE = 0.05
CHUNK = 32

F32 = jnp.float32
BF16 = jnp.bfloat16
VMEM = pl.BlockSpec(memory_space=pltpu.VMEM)
SMEM = pl.BlockSpec(memory_space=pltpu.SMEM)

FE, FO, PU, PV, FET, FOT, PUT, PVT = range(8)


def real_form(matrix):
    return np.block([[matrix.real, matrix.imag], [-matrix.imag, matrix.real]])


def tables():
    n = np.arange(HALF)
    even = np.exp(-2j * np.pi * ((2 * np.outer(n, n)) % PROBE) / PROBE) / math_root()
    odd = np.exp(-2j * np.pi * ((n[:, None] * (2 * n[None, :] + 1)) % PROBE) / PROBE) / math_root()
    whole = np.arange(PROBE)
    frequency = ((whole + HALF) % PROBE - HALF) / PROBE
    response = np.exp(-1j * np.pi * FRESNEL * frequency**2)
    first = np.fft.ifft(response)
    circulant = first[(whole[:, None] - whole[None, :]) % PROBE]
    near, far = circulant[:HALF, :HALF], circulant[:HALF, HALF:]
    forms = [real_form(m) for m in (even, odd, (near + far) / 2, (near - far) / 2)]
    forms = np.stack(forms + [m.T for m in forms]).astype(np.float32)
    high = forms.astype(BF16)
    low = (forms - high.astype(np.float32)).astype(BF16)
    return np.concatenate([high, low])


def math_root():
    return float(np.sqrt(PROBE))


def order_table():
    order = np.concatenate([np.arange(0, PROBE, 2), np.arange(1, PROBE, 2)])
    table = np.zeros((PROBE, PROBE), np.float32)
    table[order, np.arange(PROBE)] = 1.0
    return np.stack([table, table.T]).astype(BF16)


def dot(left, right):
    return jnp.dot(left, right, preferred_element_type=F32)


def parts(values):
    high = values.astype(BF16)
    low = (values - high.astype(F32)).astype(BF16)
    return high, low


def right_dot(values, tab, number):
    high, low = parts(values)
    return dot(high, tab[number]) + (dot(low, tab[number]) + dot(high, tab[number + 8]))


def left_dot(tab, number, values):
    high, low = parts(values)
    return dot(tab[number], high) + (dot(tab[number + 8], high) + dot(tab[number], low))


def halves(values, axis):
    if axis == 1:
        return values[:, :HALF], values[:, HALF:]
    return values[:HALF, :], values[HALF:, :]


def pass_along(real, imag, axis, tab, first, second, before, after):
    r0, r1 = halves(real, axis)
    i0, i1 = halves(imag, axis)
    if before:
        r0, r1, i0, i1 = r0 + r1, r0 - r1, i0 + i1, i0 - i1
    u = jnp.concatenate([r0, i0], axis=axis)
    v = jnp.concatenate([r1, i1], axis=axis)
    if axis == 1:
        u, v = right_dot(u, tab, first), right_dot(v, tab, second)
    else:
        u, v = left_dot(tab, first, u), left_dot(tab, second, v)
    r0, i0 = halves(u, axis)
    r1, i1 = halves(v, axis)
    if after:
        r0, r1, i0, i1 = r0 + r1, r0 - r1, i0 + i1, i0 - i1
    return jnp.concatenate([r0, r1], axis=axis), jnp.concatenate([i0, i1], axis=axis)


def outside(shape, axis, base, offset):
    place = lax.broadcasted_iota(jnp.int32, shape, axis) + base
    start = offset - HALF
    return (place < start) | (place >= start + PROBE)


def prepare_kernel(offs, probe, intensity, order, rolled, ordered, work):
    for slot in range(SLOTS):
        for part in range(2):
            value = pltpu.roll(probe[part], (offs[2 * slot] + HALF) & (PROBE - 1), 0)
            rolled[slot, part] = pltpu.roll(value, (offs[2 * slot + 1] + HALF) & (PROBE - 1), 1)
    for slot in range(SLOTS):
        value = intensity[slot]
        for axis in (1, 0):
            high = value.astype(BF16)
            rest = value - high.astype(F32)
            middle = rest.astype(BF16)
            low = (rest - middle.astype(F32)).astype(BF16)
            if axis == 1:
                value = (dot(high, order[0]) + dot(middle, order[0])) + dot(low, order[0])
                work[...] = value
                value = work[...]
            else:
                value = (dot(order[1], high) + dot(order[1], middle)) + dot(order[1], low)
        ordered[slot] = value


def gather_windows(offs, wide, row_a, row_b, slice_number, target):
    parity = offs[2 * SLOTS + 1]
    for source, half in ((row_a, parity), (row_b, 1 - parity)):

        @pl.loop(0, HALF // CHUNK)
        def _(step):
            start = pl.multiple_of(step * CHUNK, CHUNK)
            base = pl.multiple_of(half * HALF + start, CHUNK)
            for slot in range(SLOTS):
                shape = (CHUNK, PROBE)
                row_out = outside(shape, 0, base, offs[2 * slot])
                col_out = outside(shape, 1, 0, offs[2 * slot + 1])
                for part in range(2):
                    channel = 2 * slice_number + part
                    own = wide[channel, pl.ds(base, CHUNK), :]
                    other = source[channel, pl.ds(start, CHUNK), :]
                    near = jnp.where(row_out, other[:, :PROBE], own[:, :PROBE])
                    across = jnp.where(row_out, other[:, PROBE:], own[:, PROBE:])
                    target[slot, part, pl.ds(base, CHUNK), :] = jnp.where(col_out, across, near)


def spread(offs, contrib, slice_number, kept, send_a, send_b):
    parity = offs[2 * SLOTS + 1]
    for target, half in ((send_a, parity), (send_b, 1 - parity)):

        @pl.loop(0, HALF // CHUNK)
        def _(step):
            start = pl.multiple_of(step * CHUNK, CHUNK)
            base = pl.multiple_of(half * HALF + start, CHUNK)
            shape = (CHUNK, PROBE)
            masks = [
                (outside(shape, 0, base, offs[2 * s]), outside(shape, 1, 0, offs[2 * s + 1]))
                for s in range(SLOTS)
            ]
            for part in range(2):
                channel = 2 * slice_number + part
                totals = [None] * 4
                for slot, (row_out, col_out) in enumerate(masks):
                    value = contrib[slot, part, pl.ds(base, CHUNK), :]
                    zero = jnp.zeros_like(value)
                    inner = jnp.where(row_out, zero, value)
                    outer = jnp.where(row_out, value, zero)
                    pieces = [
                        jnp.where(col_out, zero, inner),
                        jnp.where(col_out, inner, zero),
                        jnp.where(col_out, zero, outer),
                        jnp.where(col_out, outer, zero),
                    ]
                    totals = [p if t is None else t + p for t, p in zip(totals, pieces)]
                kept[channel, pl.ds(base, CHUNK), :PROBE] = totals[0]
                kept[channel, pl.ds(base, CHUNK), PROBE:] = totals[1]
                target[channel, pl.ds(start, CHUNK), :PROBE] = totals[2]
                target[channel, pl.ds(start, CHUNK), PROBE:] = totals[3]


def gradient_kernel(
    offs, wide, row_a, row_b, rolled, ordered, tab, kept, send_a, send_b, win0, win1, wave, work, held
):
    gather_windows(offs, wide, row_a, row_b, 0, win0)
    gather_windows(offs, wide, row_a, row_b, 1, win1)
    for s in range(SLOTS):
        pr, pi, wr, wi = rolled[s, 0], rolled[s, 1], win0[s, 0], win0[s, 1]
        out = pass_along(pr * wr - pi * wi, pr * wi + pi * wr, 1, tab, PU, PV, True, True)
        work[s, 0], work[s, 1] = out
    for s in range(SLOTS):
        wave[s, 0], wave[s, 1] = pass_along(
            work[s, 0], work[s, 1], 0, tab, PUT, PVT, True, True
        )
    for s in range(SLOTS):
        pr, pi, wr, wi = wave[s, 0], wave[s, 1], win1[s, 0], win1[s, 1]
        out = pass_along(pr * wr - pi * wi, pr * wi + pi * wr, 1, tab, FE, FO, True, False)
        held[s, 0], held[s, 1] = out
    for s in range(SLOTS):
        weight = jnp.where(s < offs[2 * SLOTS], 1.0, 0.0).astype(F32)
        fr, fi = pass_along(held[s, 0], held[s, 1], 0, tab, FET, FOT, True, False)
        factor = weight * (fr * fr + fi * fi - ordered[s])
        work[s, 0], work[s, 1] = factor * fr, factor * fi
    for s in range(SLOTS):
        held[s, 0], held[s, 1] = pass_along(work[s, 0], work[s, 1], 0, tab, FE, FO, False, True)
    for s in range(SLOTS):
        br, bi = pass_along(held[s, 0], held[s, 1], 1, tab, FET, FOT, False, True)
        er, ei, wr, wi = wave[s, 0], wave[s, 1], win1[s, 0], win1[s, 1]
        wave[s, 0], wave[s, 1] = er * br + ei * bi, er * bi - ei * br
        work[s, 0], work[s, 1] = wr * br + wi * bi, wr * bi - wi * br
    spread(offs, wave, 1, kept, send_a, send_b)
    for s in range(SLOTS):
        held[s, 0], held[s, 1] = pass_along(work[s, 0], work[s, 1], 1, tab, PUT, PVT, True, True)
    for s in range(SLOTS):
        br, bi = pass_along(held[s, 0], held[s, 1], 0, tab, PU, PV, True, True)
        pr, pi = rolled[s, 0], rolled[s, 1]
        work[s, 0], work[s, 1] = pr * br + pi * bi, pr * bi - pi * br
    spread(offs, work, 0, kept, send_a, send_b)


def copy_rows(parity, wide, send_a, send_b, write=None):
    for target, half in ((send_a, 1 - parity), (send_b, parity)):

        @pl.loop(0, HALF // CHUNK)
        def _(step):
            start = pl.multiple_of(step * CHUNK, CHUNK)
            base = pl.multiple_of(half * HALF + start, CHUNK)
            for channel in range(CHANNELS):
                target[channel, pl.ds(start, CHUNK), :] = write(channel, base)


def widen_kernel(offs, own, right, left, wide, send_a, send_b):
    def write(channel, base):
        rows = pl.ds(base, CHUNK)
        value = jnp.concatenate(
            [own[channel, rows, :], right[channel, rows, :], left[channel, rows, :]], axis=1
        )
        wide[channel, rows, :] = value
        return value

    copy_rows(offs[2 * SLOTS + 1], wide, send_a, send_b, write)


def fold_rows(offs, kept, row_a, row_b, write):
    parity = offs[2 * SLOTS + 1]
    for source, half in ((row_a, 1 - parity), (row_b, parity)):

        @pl.loop(0, HALF // CHUNK)
        def _(step):
            start = pl.multiple_of(step * CHUNK, CHUNK)
            base = pl.multiple_of(half * HALF + start, CHUNK)
            for channel in range(CHANNELS):
                value = kept[channel, pl.ds(base, CHUNK), :] + source[channel, pl.ds(start, CHUNK), :]
                write(channel, pl.ds(base, CHUNK), value)


def fold_middle_kernel(offs, kept, row_a, row_b, total, to_right, to_left):
    def write(channel, rows, value):
        total[channel, rows, :] = value
        to_right[channel, rows, :HALF] = value[:, 256:384]
        to_right[channel, rows, HALF:] = value[:, 128:256]
        to_left[channel, rows, :HALF] = value[:, 0:128]
        to_left[channel, rows, HALF:] = value[:, 384:512]

    fold_rows(offs, kept, row_a, row_b, write)


def fold_last_kernel(offs, kept, row_a, row_b, total, to_right, to_left):
    def write(channel, rows, value):
        total[channel, rows, :] = value[:, :256]
        to_right[channel, rows, :] = value[:, 256:384]
        to_left[channel, rows, :] = value[:, 384:512]

    fold_rows(offs, kept, row_a, row_b, write)


def update_middle_kernel(offs, wide, total, from_left, from_right, after, send_a, send_b):
    def write(channel, base):
        rows = pl.ds(base, CHUNK)
        low, high = from_left[channel, rows, :], from_right[channel, rows, :]
        came = jnp.concatenate(
            [low[:, :HALF], high[:, HALF:], high[:, :HALF], low[:, HALF:]], axis=1
        )
        value = wide[channel, rows, :] - STEP_SIZE * (total[channel, rows, :] + came)
        after[channel, rows, :] = value
        return value

    copy_rows(offs[2 * SLOTS + 1], wide, send_a, send_b, write)


def update_last_kernel(wide, total, from_left, from_right, after):
    @pl.loop(0, PROBE // CHUNK)
    def _(step):
        rows = pl.ds(pl.multiple_of(step * CHUNK, CHUNK), CHUNK)
        for channel in range(CHANNELS):
            came = jnp.concatenate(
                [from_left[channel, rows, :], from_right[channel, rows, :]], axis=1
            )
            after[channel, rows, :] = wide[channel, rows, :PROBE] - STEP_SIZE * (
                total[channel, rows, :] + came
            )


def kernel_call(body, outs, ins, scratch=(), flops=0):
    return pl.pallas_call(
        body,
        out_shape=[jax.ShapeDtypeStruct(shape, F32) for shape in outs],
        in_specs=[SMEM if kind == "s" else VMEM for kind in ins],
        out_specs=[VMEM] * len(outs),
        scratch_shapes=[pltpu.VMEM(shape, F32) for shape in scratch],
        compiler_params=pltpu.CompilerParams(vmem_limit_bytes=56 * 1024 * 1024),
        cost_estimate=pl.CostEstimate(
            flops=flops, bytes_accessed=4 * sum(int(np.prod(s)) for s in outs), transcendentals=0
        ),
    )


WIDE = (CHANNELS, PROBE, 2 * PROBE)
BAND = (CHANNELS, HALF, 2 * PROBE)
STRIP = (CHANNELS, PROBE, HALF)
CORE = (CHANNELS, PROBE, PROBE)
FIELD = (SLOTS, 2, PROBE, PROBE)


def shifted(value, axis, steps):
    count = lax.axis_size(axis)
    return lax.ppermute(value, axis, [(i, (i + steps) % count) for i in range(count)])


def swapped(value, axis, odd):
    count = lax.axis_size(axis)
    pairs = []
    for low in range(odd, count + odd, 2):
        one, two = low % count, (low + 1) % count
        pairs += [(one, two), (two, one)]
    return lax.ppermute(value, axis, pairs)


def local(object_core, probe_field, offsets, tile_counts, intensity):
    parity = lax.axis_index("row") % 2
    scalars = jnp.concatenate(
        [offsets.reshape(-1), tile_counts.reshape(-1), parity.astype(jnp.int32).reshape(1)]
    )
    tab = jnp.asarray(tables())
    order = jnp.asarray(order_table())

    right = shifted(object_core[:, :, :HALF], "col", -1)
    left = shifted(object_core[:, :, HALF:], "col", 1)
    rolled, ordered = kernel_call(
        prepare_kernel, [FIELD, (SLOTS, PROBE, PROBE)], "svvv", [(PROBE, PROBE)], 10**9
    )(scalars, probe_field, intensity[0, 0], order)
    wide, send_a, send_b = kernel_call(widen_kernel, [WIDE, BAND, BAND], "svvv", flops=10**7)(
        scalars, object_core, right, left
    )
    for iteration in range(ITERS):
        row_b = swapped(send_b, "row", 1)
        row_a = swapped(send_a, "row", 0)
        kept, send_a, send_b = kernel_call(
            gradient_kernel,
            [WIDE, BAND, BAND],
            "svvvvvv",
            [FIELD] * 5,
            10**10,
        )(scalars, wide, row_a, row_b, rolled, ordered, tab)
        row_b = swapped(send_b, "row", 1)
        row_a = swapped(send_a, "row", 0)
        last = iteration == ITERS - 1
        if last:
            total, to_right, to_left = kernel_call(
                fold_last_kernel, [CORE, STRIP, STRIP], "svvv", flops=10**7
            )(scalars, kept, row_a, row_b)
        else:
            total, to_right, to_left = kernel_call(
                fold_middle_kernel, [WIDE, CORE, CORE], "svvv", flops=10**7
            )(scalars, kept, row_a, row_b)
        from_left = shifted(to_right, "col", 1)
        from_right = shifted(to_left, "col", -1)
        if last:
            (after,) = kernel_call(update_last_kernel, [CORE], "vvvv", flops=10**7)(
                wide, total, from_left, from_right
            )
            return after
        wide, send_a, send_b = kernel_call(
            update_middle_kernel, [WIDE, BAND, BAND], "svvvv", flops=10**7
        )(scalars, wide, total, from_left, from_right)


def solution(mesh):
    placed = (
        P(None, "row", "col"),
        P(),
        P("row", "col", None, None),
        P("row", "col"),
        P("row", "col", None, None, None),
    )
    return jax.shard_map(
        local, mesh=mesh, in_specs=placed, out_specs=P(None, "row", "col"), check_vma=False
    )
```

profile of v0, /device:TPU:0, one launch (start us, length us, event | category | flops | bytes accessed | tf_op | source)
XLA Modules:
  0.0 183.2 jit_solution(14694967070847554306)
XLA Ops:
  0.0 1.3 fusion
  1.3 2.1 %collective-permute-start.1 = (f32[4,256,128]{2,1,0:T(8,128)S(1)}, f32[4,256,128]{2,1,0:T(8,128)S(1)}, u32[]{:S(2)}, u32[]{:S(2)}) collective-permute-start(f32[4,256,128]{2,1,0:T(8,128)S(1)} %get-tuple-element.45), channel_id=1, source_target_pairs={{0,1},{1,2},{2,3},{3,4},{4,5},{5,6},{6,7},{7,0},{8,9},{9,10},{10,1... | collective-permute-start | bytes 1572872 | tf_op jit(solution)/shard_map/ppermute | solution.py:332
  3.4 3.1 %collective-permute-start = (f32[4,256,128]{2,1,0:T(8,128)S(1)}, f32[4,256,128]{2,1,0:T(8,128)S(1)}, u32[]{:S(2)}, u32[]{:S(2)}) collective-permute-start(f32[4,256,128]{2,1,0:T(8,128)S(1)} %get-tuple-element.46), channel_id=1, source_target_pairs={{0,7},{1,0},{2,1},{3,2},{4,3},{5,4},{6,5},{7,6},{8,15},{9,8},{10,9... | collective-permute-start | bytes 1572872 | tf_op jit(solution)/shard_map/ppermute | solution.py:332
  7.9 10.4 %collective-permute-done.1.left = f32[4,256,128]{2,1,0:T(8,128)S(1)} collective-permute-done((f32[4,256,128]{2,1,0:T(8,128)S(1)}, f32[4,256,128]{2,1,0:T(8,128)S(1)}, u32[]{:S(2)}, u32[]{:S(2)}) %collective-permute-start.1) | collective-permute-done | bytes 524320 | tf_op jit(solution)/shard_map/ppermute | solution.py:332
  18.4 0.8 copy-done.6
  19.2 0.8 copy-done.7
  19.9 3.8 %shard_map.73 = (f32[4,256,512]{2,1,0:T(8,128)}, f32[4,128,512]{2,1,0:T(8,128)}, f32[4,128,512]{2,1,0:T(8,128)}) custom-call(s32[8]{0:T(128)} %pad_add_fusion.offs, f32[4,256,256]{2,1,0:T(8,128)} %own.1, f32[4,256,128]{2,1,0:T(8,128)} %copy-done.7, f32[4,256,128]{2,1,0:T(8,128)} %copy-done.6), custom_call_target="tpu_custom_call" | custom-call | flops 10000000 | bytes 4194304 | tf_op jit(solution)/shard_map/pallas_call | solution.py:357
  23.8 5.3 %collective-permute-start.3 = (f32[4,128,512]{2,1,0:T(8,128)}, f32[4,128,512]{2,1,0:T(8,128)S(1)}, u32[]{:S(2)}, u32[]{:S(2)}) collective-permute-start(f32[4,128,512]{2,1,0:T(8,128)} %get-tuple-element.27), channel_id=1, source_target_pairs={{8,16},{16,8},{24,32},{32,24},{40,48},{48,40},{56,64},{64,56},{72,... | collective-permute-start | bytes 3145736 | tf_op jit(solution)/shard_map/ppermute | solution.py:341
  29.1 4.0 %shard_map.74 = (f32[3,2,256,256]{3,2,1,0:T(8,128)}, f32[3,256,256]{2,1,0:T(8,128)}) custom-call(s32[8]{0:T(128)} %pad_add_fusion.offs, f32[2,256,256]{2,1,0:T(8,128)} %probe.1, f32[3,256,256]{2,1,0:T(8,128)} %bitcast.4, bf16[2,256,256]{2,1,0:T(8,128)(2,1)} %constant.24.clone.order), custom_call_target="tpu_custom_call" | custom-call | flops 1000000000 | bytes 2359296 | tf_op jit(solution)/shard_map/pallas_call | solution.py:354
  33.0 8.8 %collective-permute-done.3.row_b = f32[4,128,512]{2,1,0:T(8,128)S(1)} collective-permute-done((f32[4,128,512]{2,1,0:T(8,128)}, f32[4,128,512]{2,1,0:T(8,128)S(1)}, u32[]{:S(2)}, u32[]{:S(2)}) %collective-permute-start.3) | collective-permute-done | bytes 1048608 | tf_op jit(solution)/shard_map/ppermute | solution.py:341
  41.8 1.0 copy-done.13
  42.9 13.0 %shard_map.75 = (f32[4,256,512]{2,1,0:T(8,128)}, f32[4,128,512]{2,1,0:T(8,128)}, f32[4,128,512]{2,1,0:T(8,128)}) custom-call(s32[8]{0:T(128)} %pad_add_fusion.offs, f32[4,256,512]{2,1,0:T(8,128)} %get-tuple-element.25.wide, f32[4,128,512]{2,1,0:T(8,128)} %copy-done.11, f32[4,128,512]{2,1,0:T(8,128)} %copy-done.13, ...), custom_call_target="tpu_custom_call" | custom-call | flops 10000000000 | bytes 4194304 | tf_op jit(solution)/shard_map/pallas_call | solution.py:363
  55.9 5.3 %collective-permute-start.5 = (f32[4,128,512]{2,1,0:T(8,128)}, f32[4,128,512]{2,1,0:T(8,128)S(1)}, u32[]{:S(2)}, u32[]{:S(2)}) collective-permute-start(f32[4,128,512]{2,1,0:T(8,128)} %get-tuple-element.32), channel_id=1, source_target_pairs={{8,16},{16,8},{24,32},{32,24},{40,48},{48,40},{56,64},{64,56},{72,... | collective-permute-start | bytes 3145736 | tf_op jit(solution)/shard_map/ppermute | solution.py:341
  61.2 12.8 %collective-permute-done.5.row_b = f32[4,128,512]{2,1,0:T(8,128)S(1)} collective-permute-done((f32[4,128,512]{2,1,0:T(8,128)}, f32[4,128,512]{2,1,0:T(8,128)S(1)}, u32[]{:S(2)}, u32[]{:S(2)}) %collective-permute-start.5) | collective-permute-done | bytes 1048608 | tf_op jit(solution)/shard_map/ppermute | solution.py:341
  73.9 1.0 copy-done.5
  75.0 4.5 %shard_map.76 = (f32[4,256,512]{2,1,0:T(8,128)}, f32[4,256,256]{2,1,0:T(8,128)}, f32[4,256,256]{2,1,0:T(8,128)}) custom-call(s32[8]{0:T(128)} %pad_add_fusion.offs, f32[4,256,512]{2,1,0:T(8,128)} %get-tuple-element.30.kept, f32[4,128,512]{2,1,0:T(8,128)} %copy-done.2, f32[4,128,512]{2,1,0:T(8,128)} %copy-done.5), custom_call_target="tpu_custom_call" | custom-call | flops 10000000 | bytes 4194304 | tf_op jit(solution)/shard_map/pallas_call | solution.py:378
  79.5 4.1 %collective-permute-start.7 = (f32[4,256,256]{2,1,0:T(8,128)}, f32[4,256,256]{2,1,0:T(8,128)S(1)}, u32[]{:S(2)}, u32[]{:S(2)}) collective-permute-start(f32[4,256,256]{2,1,0:T(8,128)} %get-tuple-element.35), channel_id=1, source_target_pairs={{0,7},{1,0},{2,1},{3,2},{4,3},{5,4},{6,5},{7,6},{8,15},{9,8},{10,9... | collective-permute-start | bytes 3145736 | tf_op jit(solution)/shard_map/ppermute | solution.py:332
  83.6 20.4 %collective-permute-done.6.from_left = f32[4,256,256]{2,1,0:T(8,128)S(1)} collective-permute-done((f32[4,256,256]{2,1,0:T(8,128)}, f32[4,256,256]{2,1,0:T(8,128)S(1)}, u32[]{:S(2)}, u32[]{:S(2)}) %collective-permute-start.6) | collective-permute-done | bytes 1048608 | tf_op jit(solution)/shard_map/ppermute | solution.py:332
  104.1 1.0 copy-done
  105.4 5.2 %shard_map.77 = (f32[4,256,512]{2,1,0:T(8,128)}, f32[4,128,512]{2,1,0:T(8,128)}, f32[4,128,512]{2,1,0:T(8,128)}) custom-call(s32[8]{0:T(128)} %pad_add_fusion.offs, f32[4,256,512]{2,1,0:T(8,128)} %get-tuple-element.25.wide, f32[4,256,512]{2,1,0:T(8,128)} %get-tuple-element.33.total, f32[4,256,256]{2,1,0:T(8,128)} %copy-done, f32[4,256,256]{2,1,0:T(8,128)} %copy-done.3), custom_call_target="tpu_custom_call" | custom-call | flops 10000000 | bytes 4194304 | tf_op jit(solution)/shard_map/pallas_call | solution.py:388
  110.6 5.3 %collective-permute-start.9 = (f32[4,128,512]{2,1,0:T(8,128)}, f32[4,128,512]{2,1,0:T(8,128)S(1)}, u32[]{:S(2)}, u32[]{:S(2)}) collective-permute-start(f32[4,128,512]{2,1,0:T(8,128)} %get-tuple-element.38), channel_id=1, source_target_pairs={{8,16},{16,8},{24,32},{32,24},{40,48},{48,40},{56,64},{64,56},{72,... | collective-permute-start | bytes 3145736 | tf_op jit(solution)/shard_map/ppermute | solution.py:341
  115.9 12.8 %collective-permute-done.9.row_b = f32[4,128,512]{2,1,0:T(8,128)S(1)} collective-permute-done((f32[4,128,512]{2,1,0:T(8,128)}, f32[4,128,512]{2,1,0:T(8,128)S(1)}, u32[]{:S(2)}, u32[]{:S(2)}) %collective-permute-start.9) | collective-permute-done | bytes 1048608 | tf_op jit(solution)/shard_map/ppermute | solution.py:341
  128.7 1.0 copy-done.14
  129.7 13.0 %shard_map.78 = (f32[4,256,512]{2,1,0:T(8,128)}, f32[4,128,512]{2,1,0:T(8,128)}, f32[4,128,512]{2,1,0:T(8,128)}) custom-call(s32[8]{0:T(128)} %pad_add_fusion.offs, f32[4,256,512]{2,1,0:T(8,128)} %get-tuple-element.36.wide, f32[4,128,512]{2,1,0:T(8,128)} %copy-done.12, f32[4,128,512]{2,1,0:T(8,128)} %copy-done.14, ...), custom_call_target="tpu_custom_call" | custom-call | flops 10000000000 | bytes 4194304 | tf_op jit(solution)/shard_map/pallas_call | solution.py:363
  142.8 5.3 %collective-permute-start.11 = (f32[4,128,512]{2,1,0:T(8,128)}, f32[4,128,512]{2,1,0:T(8,128)S(1)}, u32[]{:S(2)}, u32[]{:S(2)}) collective-permute-start(f32[4,128,512]{2,1,0:T(8,128)} %get-tuple-element.41), channel_id=1, source_target_pairs={{8,16},{16,8},{24,32},{32,24},{40,48},{48,40},{56,64},{64,56},{72,... | collective-permute-start | bytes 3145736 | tf_op jit(solution)/shard_map/ppermute | solution.py:341
  148.0 12.8 %collective-permute-done.11.row_b = f32[4,128,512]{2,1,0:T(8,128)S(1)} collective-permute-done((f32[4,128,512]{2,1,0:T(8,128)}, f32[4,128,512]{2,1,0:T(8,128)S(1)}, u32[]{:S(2)}, u32[]{:S(2)}) %collective-permute-start.11) | collective-permute-done | bytes 1048608 | tf_op jit(solution)/shard_map/ppermute | solution.py:341
  160.8 1.0 copy-done.4
  161.8 3.8 %shard_map.79 = (f32[4,256,256]{2,1,0:T(8,128)}, f32[4,256,128]{2,1,0:T(8,128)}, f32[4,256,128]{2,1,0:T(8,128)}) custom-call(s32[8]{0:T(128)} %pad_add_fusion.offs, f32[4,256,512]{2,1,0:T(8,128)} %get-tuple-element.39.kept, f32[4,128,512]{2,1,0:T(8,128)} %copy-done.1, f32[4,128,512]{2,1,0:T(8,128)} %copy-done.4), custom_call_target="tpu_custom_call" | custom-call | flops 10000000 | bytes 2097152 | tf_op jit(solution)/shard_map/pallas_call | solution.py:374
  165.6 4.1 %collective-permute-start.13 = (f32[4,256,128]{2,1,0:T(8,128)}, f32[4,256,128]{2,1,0:T(8,128)S(1)}, u32[]{:S(2)}, u32[]{:S(2)}) collective-permute-start(f32[4,256,128]{2,1,0:T(8,128)} %get-tuple-element.44), channel_id=1, source_target_pairs={{0,7},{1,0},{2,1},{3,2},{4,3},{5,4},{6,5},{7,6},{8,15},{9,8},{10,9... | collective-permute-start | bytes 1572872 | tf_op jit(solution)/shard_map/ppermute | solution.py:332
  169.7 9.2 %collective-permute-done.12.from_left = f32[4,256,128]{2,1,0:T(8,128)S(1)} collective-permute-done((f32[4,256,128]{2,1,0:T(8,128)}, f32[4,256,128]{2,1,0:T(8,128)S(1)}, u32[]{:S(2)}, u32[]{:S(2)}) %collective-permute-start.12) | collective-permute-done | bytes 524320 | tf_op jit(solution)/shard_map/ppermute | solution.py:332
  178.9 0.8 copy-done.8
  179.9 3.3 %shard_map.80 = f32[4,256,256]{2,1,0:T(8,128)} custom-call(f32[4,256,512]{2,1,0:T(8,128)} %get-tuple-element.36.wide, f32[4,256,256]{2,1,0:T(8,128)} %get-tuple-element.42.total, f32[4,256,128]{2,1,0:T(8,128)} %copy-done.8, f32[4,256,128]{2,1,0:T(8,128)} %copy-done.9), custom_call_target="tpu_custom_call" | custom-call | flops 10000000 | bytes 1048576 | tf_op jit(solution)/shard_map/pallas_call | solution.py:384
  (38 shorter events, 1.4 us)
Async XLA Ops:
  0.0 7.2 %copy-start.10 = (s32[1,1,3,2]{2,3,1,0:T(2,128)S(1)}, s32[1,1,3,2]{2,3,1,0:T(2,128)}, u32[]{:S(2)}) copy-start(s32[1,1,3,2]{2,3,1,0:T(2,128)} %param.9) | copy-start | bytes 76
  1.3 17.1 %collective-permute-start.1 = (f32[4,256,128]{2,1,0:T(8,128)S(1)}, f32[4,256,128]{2,1,0:T(8,128)S(1)}, u32[]{:S(2)}, u32[]{:S(2)}) collective-permute-start(f32[4,256,128]{2,1,0:T(8,128)S(1)} %get-tuple-element.45), channel_id=1, source_target_pairs={{0,1},{1,2},{2,3},{3,4},{4,5},{5,6},{6,7},{7,0},{8,9},{9,10},{10,1... | collective-permute-start | bytes 1572872 | tf_op jit(solution)/shard_map/ppermute | solution.py:332
  3.4 15.0 %collective-permute-start = (f32[4,256,128]{2,1,0:T(8,128)S(1)}, f32[4,256,128]{2,1,0:T(8,128)S(1)}, u32[]{:S(2)}, u32[]{:S(2)}) collective-permute-start(f32[4,256,128]{2,1,0:T(8,128)S(1)} %get-tuple-element.46), channel_id=1, source_target_pairs={{0,7},{1,0},{2,1},{3,2},{4,3},{5,4},{6,5},{7,6},{8,15},{9,8},{10,9... | collective-permute-start | bytes 1572872 | tf_op jit(solution)/shard_map/ppermute | solution.py:332
  18.4 0.8 copy-start.6
  19.2 0.8 copy-start.7
  23.8 9.3 %collective-permute-start.2 = (f32[4,128,512]{2,1,0:T(8,128)}, f32[4,128,512]{2,1,0:T(8,128)S(1)}, u32[]{:S(2)}, u32[]{:S(2)}) collective-permute-start(f32[4,128,512]{2,1,0:T(8,128)} %get-tuple-element.26), channel_id=1, source_target_pairs={{0,8},{8,0},{16,24},{24,16},{32,40},{40,32},{48,56},{56,48},{64,72... | collective-permute-start | bytes 3145736 | tf_op jit(solution)/shard_map/ppermute | solution.py:341
  23.8 18.0 %collective-permute-start.3 = (f32[4,128,512]{2,1,0:T(8,128)}, f32[4,128,512]{2,1,0:T(8,128)S(1)}, u32[]{:S(2)}, u32[]{:S(2)}) collective-permute-start(f32[4,128,512]{2,1,0:T(8,128)} %get-tuple-element.27), channel_id=1, source_target_pairs={{8,16},{16,8},{24,32},{32,24},{40,48},{48,40},{56,64},{64,56},{72,... | collective-permute-start | bytes 3145736 | tf_op jit(solution)/shard_map/ppermute | solution.py:341
  33.0 8.8 %copy-start.11 = (f32[4,128,512]{2,1,0:T(8,128)}, f32[4,128,512]{2,1,0:T(8,128)S(1)}, u32[]{:S(2)}) copy-start(f32[4,128,512]{2,1,0:T(8,128)S(1)} %collective-permute-done.2.row_a) | copy-start | bytes 3145732
  41.8 1.0 copy-start.13
  55.9 5.3 %collective-permute-start.4 = (f32[4,128,512]{2,1,0:T(8,128)}, f32[4,128,512]{2,1,0:T(8,128)S(1)}, u32[]{:S(2)}, u32[]{:S(2)}) collective-permute-start(f32[4,128,512]{2,1,0:T(8,128)} %get-tuple-element.31), channel_id=1, source_target_pairs={{0,8},{8,0},{16,24},{24,16},{32,40},{40,32},{48,56},{56,48},{64,72... | collective-permute-start | bytes 3145736 | tf_op jit(solution)/shard_map/ppermute | solution.py:341
  55.9 18.0 %collective-permute-start.5 = (f32[4,128,512]{2,1,0:T(8,128)}, f32[4,128,512]{2,1,0:T(8,128)S(1)}, u32[]{:S(2)}, u32[]{:S(2)}) collective-permute-start(f32[4,128,512]{2,1,0:T(8,128)} %get-tuple-element.32), channel_id=1, source_target_pairs={{8,16},{16,8},{24,32},{32,24},{40,48},{48,40},{56,64},{64,56},{72,... | collective-permute-start | bytes 3145736 | tf_op jit(solution)/shard_map/ppermute | solution.py:341
  61.2 12.8 %copy-start.2 = (f32[4,128,512]{2,1,0:T(8,128)}, f32[4,128,512]{2,1,0:T(8,128)S(1)}, u32[]{:S(2)}) copy-start(f32[4,128,512]{2,1,0:T(8,128)S(1)} %collective-permute-done.4.row_a) | copy-start | bytes 3145732
  73.9 1.0 copy-start.5
  79.5 24.6 %collective-permute-start.6 = (f32[4,256,256]{2,1,0:T(8,128)}, f32[4,256,256]{2,1,0:T(8,128)S(1)}, u32[]{:S(2)}, u32[]{:S(2)}) collective-permute-start(f32[4,256,256]{2,1,0:T(8,128)} %get-tuple-element.34), channel_id=1, source_target_pairs={{0,1},{1,2},{2,3},{3,4},{4,5},{5,6},{6,7},{7,0},{8,9},{9,10},{10,1... | collective-permute-start | bytes 3145736 | tf_op jit(solution)/shard_map/ppermute | solution.py:332
  79.5 24.6 %collective-permute-start.7 = (f32[4,256,256]{2,1,0:T(8,128)}, f32[4,256,256]{2,1,0:T(8,128)S(1)}, u32[]{:S(2)}, u32[]{:S(2)}) collective-permute-start(f32[4,256,256]{2,1,0:T(8,128)} %get-tuple-element.35), channel_id=1, source_target_pairs={{0,7},{1,0},{2,1},{3,2},{4,3},{5,4},{6,5},{7,6},{8,15},{9,8},{10,9... | collective-permute-start | bytes 3145736 | tf_op jit(solution)/shard_map/ppermute | solution.py:332
  104.1 1.0 copy-start
  104.1 1.4 copy-start.3
  110.6 5.3 %collective-permute-start.8 = (f32[4,128,512]{2,1,0:T(8,128)}, f32[4,128,512]{2,1,0:T(8,128)S(1)}, u32[]{:S(2)}, u32[]{:S(2)}) collective-permute-start(f32[4,128,512]{2,1,0:T(8,128)} %get-tuple-element.37), channel_id=1, source_target_pairs={{0,8},{8,0},{16,24},{24,16},{32,40},{40,32},{48,56},{56,48},{64,72... | collective-permute-start | bytes 3145736 | tf_op jit(solution)/shard_map/ppermute | solution.py:341
  110.6 18.0 %collective-permute-start.9 = (f32[4,128,512]{2,1,0:T(8,128)}, f32[4,128,512]{2,1,0:T(8,128)S(1)}, u32[]{:S(2)}, u32[]{:S(2)}) collective-permute-start(f32[4,128,512]{2,1,0:T(8,128)} %get-tuple-element.38), channel_id=1, source_target_pairs={{8,16},{16,8},{24,32},{32,24},{40,48},{48,40},{56,64},{64,56},{72,... | collective-permute-start | bytes 3145736 | tf_op jit(solution)/shard_map/ppermute | solution.py:341
  115.9 12.8 %copy-start.12 = (f32[4,128,512]{2,1,0:T(8,128)}, f32[4,128,512]{2,1,0:T(8,128)S(1)}, u32[]{:S(2)}) copy-start(f32[4,128,512]{2,1,0:T(8,128)S(1)} %collective-permute-done.8.row_a) | copy-start | bytes 3145732
  128.7 1.0 copy-start.14
  142.8 5.3 %collective-permute-start.10 = (f32[4,128,512]{2,1,0:T(8,128)}, f32[4,128,512]{2,1,0:T(8,128)S(1)}, u32[]{:S(2)}, u32[]{:S(2)}) collective-permute-start(f32[4,128,512]{2,1,0:T(8,128)} %get-tuple-element.40), channel_id=1, source_target_pairs={{0,8},{8,0},{16,24},{24,16},{32,40},{40,32},{48,56},{56,48},{64,72... | collective-permute-start | bytes 3145736 | tf_op jit(solution)/shard_map/ppermute | solution.py:341
  142.8 18.0 %collective-permute-start.11 = (f32[4,128,512]{2,1,0:T(8,128)}, f32[4,128,512]{2,1,0:T(8,128)S(1)}, u32[]{:S(2)}, u32[]{:S(2)}) collective-permute-start(f32[4,128,512]{2,1,0:T(8,128)} %get-tuple-element.41), channel_id=1, source_target_pairs={{8,16},{16,8},{24,32},{32,24},{40,48},{48,40},{56,64},{64,56},{72,... | collective-permute-start | bytes 3145736 | tf_op jit(solution)/shard_map/ppermute | solution.py:341
  148.0 12.8 %copy-start.1 = (f32[4,128,512]{2,1,0:T(8,128)}, f32[4,128,512]{2,1,0:T(8,128)S(1)}, u32[]{:S(2)}) copy-start(f32[4,128,512]{2,1,0:T(8,128)S(1)} %collective-permute-done.10.row_a) | copy-start | bytes 3145732
  160.8 1.0 copy-start.4
  165.6 13.3 %collective-permute-start.12 = (f32[4,256,128]{2,1,0:T(8,128)}, f32[4,256,128]{2,1,0:T(8,128)S(1)}, u32[]{:S(2)}, u32[]{:S(2)}) collective-permute-start(f32[4,256,128]{2,1,0:T(8,128)} %get-tuple-element.43), channel_id=1, source_target_pairs={{0,1},{1,2},{2,3},{3,4},{4,5},{5,6},{6,7},{7,0},{8,9},{9,10},{10,1... | collective-permute-start | bytes 1572872 | tf_op jit(solution)/shard_map/ppermute | solution.py:332
  165.6 13.3 %collective-permute-start.13 = (f32[4,256,128]{2,1,0:T(8,128)}, f32[4,256,128]{2,1,0:T(8,128)S(1)}, u32[]{:S(2)}, u32[]{:S(2)}) collective-permute-start(f32[4,256,128]{2,1,0:T(8,128)} %get-tuple-element.44), channel_id=1, source_target_pairs={{0,7},{1,0},{2,1},{3,2},{4,3},{5,4},{6,5},{7,6},{8,15},{9,8},{10,9... | collective-permute-start | bytes 1572872 | tf_op jit(solution)/shard_map/ppermute | solution.py:332
  178.9 0.8 copy-start.8
  178.9 1.0 copy-start.9
where the time goes:
time: 184 us; the launch traced here: 183 us
  waiting for transfers between devices  87.2 us (47%)
  Pallas kernels  50.6 us (28%)
  starting transfers between devices  34.6 us (19%)
  local copies, waits for them, and re-layouts  9.54 us (5%)
    ppermute x8, waiting for transfers between devices, swapped(): return lax.ppermute(value, axis, pairs)  47.1 us
    ppermute x6, waiting for transfers between devices, shifted(): lax.ppermute(value, axis, [(i, (i + steps) % count) for i in range(count)])  40.1 us
    pallas_call x2, Pallas kernels, local(): kernel_call(gradient_kernel, [WIDE, BAND, BAND], 'svvvvvv', [FIELD] * 5,...  26 us
    ppermute x8, starting transfers between devices, swapped(): return lax.ppermute(value, axis, pairs)  21.1 us
    ppermute x6, starting transfers between devices, shifted(): lax.ppermute(value, axis, [(i, (i + steps) % count) for i in range(count)])  13.5 us
    unnamed x31, local copies, waits for them, and re-layouts  8.17 us
    pallas_call x1, Pallas kernels, local(): kernel_call(update_middle_kernel, [WIDE, BAND, BAND], 'svvvv', flops=10 *...  5.18 us
    pallas_call x1, Pallas kernels, local(): kernel_call(fold_middle_kernel, [WIDE, CORE, CORE], 'svvv', flops=10 ** 7)  4.53 us
  transfers between devices with their start and end apart: 14, of which 7 were waited for; matrix products, arithmetic and copies ran while one was open for 0% of the time, Pallas kernels for 2%

commit v1 on v0

v1 whole, which is shorter than its diff:
```python
import functools

import jax
import jax.numpy as jnp
import numpy as np
from jax import lax
from jax.experimental import pallas as pl
from jax.experimental.pallas import tpu as pltpu
from jax.sharding import PartitionSpec as P

PROBE = 256
HALF = 128
SLICES = 2
SLOTS = 3
ITERS = 2
CHANNELS = 2 * SLICES
FRESNEL = 24.0
STEP_SIZE = 0.05
CHUNK = 32

F32 = jnp.float32
BF16 = jnp.bfloat16
VMEM = pl.BlockSpec(memory_space=pltpu.VMEM)
SMEM = pl.BlockSpec(memory_space=pltpu.SMEM)

E, O, ET, OT = range(4)


def real_form(matrix):
    return np.block([[matrix.real, matrix.imag], [-matrix.imag, matrix.real]])


def stack_of(one, two):
    forms = [real_form(one), real_form(two)]
    forms = np.stack(forms + [m.T for m in forms]).astype(np.float32)
    high = forms.astype(BF16)
    low = (forms - high.astype(np.float32)).astype(BF16)
    return np.concatenate([high, low])


def tables():
    n = np.arange(HALF)
    even = np.exp(-2j * np.pi * ((2 * np.outer(n, n)) % PROBE) / PROBE) / math_root()
    odd = np.exp(-2j * np.pi * ((n[:, None] * (2 * n[None, :] + 1)) % PROBE) / PROBE) / math_root()
    whole = np.arange(PROBE)
    frequency = ((whole + HALF) % PROBE - HALF) / PROBE
    response = np.exp(-1j * np.pi * FRESNEL * frequency**2)
    first = np.fft.ifft(response)
    circulant = first[(whole[:, None] - whole[None, :]) % PROBE]
    near, far = circulant[:HALF, :HALF], circulant[:HALF, HALF:]
    return stack_of(even, odd), stack_of((near + far) / 2, (near - far) / 2)


def math_root():
    return float(np.sqrt(PROBE))


def dot(left, right):
    return jnp.dot(left, right, preferred_element_type=F32)


def parts(values):
    high = values.astype(BF16)
    low = (values - high.astype(F32)).astype(BF16)
    return high, low


def right_dot(values, tab, number):
    high, low = parts(values)
    return dot(high, tab[number]) + (dot(low, tab[number]) + dot(high, tab[number + 4]))


def left_dot(tab, number, values):
    high, low = parts(values)
    return dot(tab[number], high) + (dot(tab[number + 4], high) + dot(tab[number], low))


def halves(values, axis):
    if axis == 1:
        return values[:, :HALF], values[:, HALF:]
    return values[:HALF, :], values[HALF:, :]


def pass_along(real, imag, axis, tab, first, second, before, after):
    r0, r1 = halves(real, axis)
    i0, i1 = halves(imag, axis)
    if before:
        r0, r1, i0, i1 = r0 + r1, r0 - r1, i0 + i1, i0 - i1
    u = jnp.concatenate([r0, i0], axis=axis)
    v = jnp.concatenate([r1, i1], axis=axis)
    if axis == 1:
        u, v = right_dot(u, tab, first), right_dot(v, tab, second)
    else:
        u, v = left_dot(tab, first, u), left_dot(tab, second, v)
    r0, i0 = halves(u, axis)
    r1, i1 = halves(v, axis)
    if after:
        r0, r1, i0, i1 = r0 + r1, r0 - r1, i0 + i1, i0 - i1
    return jnp.concatenate([r0, r1], axis=axis), jnp.concatenate([i0, i1], axis=axis)


def outside(shape, axis, base, offset):
    place = lax.broadcasted_iota(jnp.int32, shape, axis) + base
    start = offset - HALF
    return (place < start) | (place >= start + PROBE)


def ordering():
    row = lax.broadcasted_iota(jnp.int32, (PROBE, PROBE), 0)
    column = lax.broadcasted_iota(jnp.int32, (PROBE, PROBE), 1)
    wanted = jnp.where(column < HALF, 2 * column, 2 * column - (PROBE - 1))
    back = jnp.where(row < HALF, 2 * row, 2 * row - (PROBE - 1))
    one = jnp.where(row == wanted, 1.0, 0.0).astype(BF16)
    two = jnp.where(column == back, 1.0, 0.0).astype(BF16)
    return one, two


def prepare_kernel(offs, probe, intensity, rolled, ordered, order):
    order[0], order[1] = ordering()
    for slot in range(SLOTS):
        for part in range(2):
            value = pltpu.roll(probe[part], (offs[2 * slot] + HALF) & (PROBE - 1), 0)
            rolled[slot, part] = pltpu.roll(value, (offs[2 * slot + 1] + HALF) & (PROBE - 1), 1)

    @pl.loop(0, SLOTS)
    def _(slot):
        for axis in (1, 0):
            value = ordered[slot] if axis == 0 else intensity[slot]
            high = value.astype(BF16)
            rest = value - high.astype(F32)
            middle = rest.astype(BF16)
            low = (rest - middle.astype(F32)).astype(BF16)
            if axis == 1:
                value = (dot(high, order[0]) + dot(middle, order[0])) + dot(low, order[0])
            else:
                value = (dot(order[1], high) + dot(order[1], middle)) + dot(order[1], low)
            ordered[slot] = value


def row_halves(offs, one, two, first):
    parity = offs[2 * SLOTS + 1]
    return ((one, parity), (two, 1 - parity)) if first else ((one, 1 - parity), (two, parity))


def chunks(half):
    def run(body):
        @pl.loop(0, HALF // CHUNK)
        def _(step):
            start = pl.multiple_of(step * CHUNK, CHUNK)
            body(pl.ds(start, CHUNK), pl.multiple_of(half * HALF + start, CHUNK))

    return run


def masks_of(offs, base):
    shape = (CHUNK, PROBE)
    return [
        (outside(shape, 0, base, offs[2 * s]), outside(shape, 1, 0, offs[2 * s + 1]))
        for s in range(SLOTS)
    ]


def gather_windows(offs, wide, row_a, row_b, target):
    for source, half in row_halves(offs, row_a, row_b, True):

        @chunks(half)
        def _(part_rows, base):
            rows = pl.ds(base, CHUNK)
            for slot, (row_out, col_out) in enumerate(masks_of(offs, base)):
                for part in range(2):
                    own = wide[part, rows, :]
                    other = source[part, part_rows, :]
                    near = jnp.where(row_out, other[:, :PROBE], own[:, :PROBE])
                    across = jnp.where(row_out, other[:, PROBE:], own[:, PROBE:])
                    target[slot, part, rows, :] = jnp.where(col_out, across, near)


def spread(offs, contrib, kept, send_a, send_b):
    for target, half in row_halves(offs, send_a, send_b, True):

        @chunks(half)
        def _(part_rows, base):
            rows = pl.ds(base, CHUNK)
            masks = masks_of(offs, base)
            for part in range(2):
                totals = [None] * 4
                for slot, (row_out, col_out) in enumerate(masks):
                    value = contrib[slot, part, rows, :]
                    zero = jnp.zeros_like(value)
                    inner = jnp.where(row_out, zero, value)
                    outer = jnp.where(row_out, value, zero)
                    pieces = [
                        jnp.where(col_out, zero, inner),
                        jnp.where(col_out, inner, zero),
                        jnp.where(col_out, zero, outer),
                        jnp.where(col_out, outer, zero),
                    ]
                    totals = [p if t is None else t + p for t, p in zip(totals, pieces)]
                kept[part, rows, :PROBE] = totals[0]
                kept[part, rows, PROBE:] = totals[1]
                target[part, part_rows, :PROBE] = totals[2]
                target[part, part_rows, PROBE:] = totals[3]


def times(ar, ai, br, bi):
    return ar * br - ai * bi, ar * bi + ai * br


def conj_times(ar, ai, br, bi):
    return ar * br + ai * bi, ar * bi - ai * br


def forward_kernel(offs, wide, row_a, row_b, rolled, tab, wave, window, work):
    gather_windows(offs, wide, row_a, row_b, window)
    for s in range(SLOTS):
        value = times(rolled[s, 0], rolled[s, 1], window[s, 0], window[s, 1])
        work[s, 0], work[s, 1] = pass_along(*value, 1, tab, E, O, True, True)
    for s in range(SLOTS):
        wave[s, 0], wave[s, 1] = pass_along(work[s, 0], work[s, 1], 0, tab, ET, OT, True, True)


def middle_kernel(
    offs, wide, row_a, row_b, wave, ordered, tab, kept, send_a, send_b, back, window, work, held
):
    gather_windows(offs, wide, row_a, row_b, window)
    for s in range(SLOTS):
        value = times(wave[s, 0], wave[s, 1], window[s, 0], window[s, 1])
        held[s, 0], held[s, 1] = pass_along(*value, 1, tab, E, O, True, False)
    for s in range(SLOTS):
        weight = jnp.where(s < offs[2 * SLOTS], 1.0, 0.0).astype(F32)
        fr, fi = pass_along(held[s, 0], held[s, 1], 0, tab, ET, OT, True, False)
        factor = weight * (fr * fr + fi * fi - ordered[s])
        work[s, 0], work[s, 1] = factor * fr, factor * fi
    for s in range(SLOTS):
        held[s, 0], held[s, 1] = pass_along(work[s, 0], work[s, 1], 0, tab, E, O, False, True)
    for s in range(SLOTS):
        value = pass_along(held[s, 0], held[s, 1], 1, tab, ET, OT, False, True)
        work[s, 0], work[s, 1] = conj_times(wave[s, 0], wave[s, 1], *value)
        back[s, 0], back[s, 1] = conj_times(window[s, 0], window[s, 1], *value)
    spread(offs, work, kept, send_a, send_b)


def backward_kernel(offs, back, rolled, tab, kept, send_a, send_b, held, work):
    for s in range(SLOTS):
        held[s, 0], held[s, 1] = pass_along(back[s, 0], back[s, 1], 1, tab, ET, OT, True, True)
    for s in range(SLOTS):
        value = pass_along(held[s, 0], held[s, 1], 0, tab, E, O, True, True)
        work[s, 0], work[s, 1] = conj_times(rolled[s, 0], rolled[s, 1], *value)
    spread(offs, work, kept, send_a, send_b)


def widen_kernel(offs, own, right, left, wide, send_a, send_b):
    for target, half in row_halves(offs, send_a, send_b, False):

        @chunks(half)
        def _(part_rows, base):
            rows = pl.ds(base, CHUNK)
            for part in range(2):
                for ref, here in ((wide, rows), (target, part_rows)):
                    ref[part, here, :256] = own[part, rows, :]
                    ref[part, here, 256:384] = right[part, rows, :]
                    ref[part, here, 384:] = left[part, rows, :]


def fold_middle_kernel(offs, kept, row_a, row_b, total, to_right, to_left):
    for source, half in row_halves(offs, row_a, row_b, False):

        @chunks(half)
        def _(part_rows, base):
            rows = pl.ds(base, CHUNK)
            for part in range(2):
                value = kept[part, rows, :] + source[part, part_rows, :]
                total[part, rows, :] = value
                to_right[part, rows, :HALF] = value[:, 256:384]
                to_right[part, rows, HALF:] = value[:, 128:256]
                to_left[part, rows, :HALF] = value[:, 0:128]
                to_left[part, rows, HALF:] = value[:, 384:512]


def fold_last_kernel(offs, kept, row_a, row_b, total, to_right, to_left):
    for source, half in row_halves(offs, row_a, row_b, False):

        @chunks(half)
        def _(part_rows, base):
            rows = pl.ds(base, CHUNK)
            for part in range(2):
                value = kept[part, rows, :] + source[part, part_rows, :]
                total[part, rows, :] = value[:, :256]
                to_right[part, rows, :] = value[:, 256:384]
                to_left[part, rows, :] = value[:, 384:512]


def update_middle_kernel(offs, wide, total, from_left, from_right, after, send_a, send_b):
    for target, half in row_halves(offs, send_a, send_b, False):

        @chunks(half)
        def _(part_rows, base):
            rows = pl.ds(base, CHUNK)
            for part in range(2):
                low, high = from_left[part, rows, :], from_right[part, rows, :]
                came = jnp.concatenate(
                    [low[:, :HALF], high[:, HALF:], high[:, :HALF], low[:, HALF:]], axis=1
                )
                value = wide[part, rows, :] - STEP_SIZE * (total[part, rows, :] + came)
                after[part, rows, :] = value
                target[part, part_rows, :] = value


def updated(wide, total, from_left, from_right, part, rows):
    came = jnp.concatenate([from_left[part, rows, :], from_right[part, rows, :]], axis=1)
    return wide[part, rows, :PROBE] - STEP_SIZE * (total[part, rows, :] + came)


def update_last_kernel(wide, total, from_left, from_right, after):
    @pl.loop(0, PROBE // CHUNK)
    def _(step):
        rows = pl.ds(pl.multiple_of(step * CHUNK, CHUNK), CHUNK)
        for part in range(2):
            after[part, rows, :] = updated(wide, total, from_left, from_right, part, rows)


def finish_kernel(wide, total, from_left, from_right, other, after):
    @pl.loop(0, PROBE // CHUNK)
    def _(step):
        rows = pl.ds(pl.multiple_of(step * CHUNK, CHUNK), CHUNK)
        for part in range(2):
            after[part, rows, :] = updated(wide, total, from_left, from_right, part, rows)
            after[part + 2, rows, :] = other[part, rows, :]


WIDE = (2, PROBE, 2 * PROBE)
BAND = (2, HALF, 2 * PROBE)
STRIP = (2, PROBE, HALF)
CORE = (2, PROBE, PROBE)
FIELD = (SLOTS, 2, PROBE, PROBE)


def kernel_call(body, outs, kinds, scratch=(), mib=8, flops=10**7):
    return pl.pallas_call(
        body,
        out_shape=[jax.ShapeDtypeStruct(shape, F32) for shape in outs],
        in_specs=[SMEM if kind == "s" else VMEM for kind in kinds],
        out_specs=[VMEM] * len(outs),
        scratch_shapes=list(scratch),
        compiler_params=pltpu.CompilerParams(vmem_limit_bytes=mib * 1024 * 1024),
        cost_estimate=pl.CostEstimate(flops=flops, bytes_accessed=10**6, transcendentals=0),
    )


def shifted(value, axis, steps):
    count = lax.axis_size(axis)
    return lax.ppermute(value, axis, [(i, (i + steps) % count) for i in range(count)])


def swapped(value, axis, odd):
    count = lax.axis_size(axis)
    pairs = []
    for low in range(odd, count + odd, 2):
        one, two = low % count, (low + 1) % count
        pairs += [(one, two), (two, one)]
    return lax.ppermute(value, axis, pairs)


def swap_rows(send_a, send_b):
    row_b = swapped(send_b, "row", 1)
    return swapped(send_a, "row", 0), row_b


def local(object_core, probe_field, offsets, tile_counts, intensity):
    parity = lax.axis_index("row") % 2
    scalars = jnp.concatenate(
        [offsets.reshape(-1), tile_counts.reshape(-1), parity.astype(jnp.int32).reshape(1)]
    )
    fourier, space = (jnp.asarray(t) for t in tables())
    field = pltpu.VMEM(FIELD, F32)

    own = [object_core[2 * k : 2 * k + 2] for k in range(SLICES)]
    beside = []
    for cells in own:
        right = shifted(cells[:, :, :HALF], "col", -1)
        left = shifted(cells[:, :, HALF:], "col", 1)
        beside.append((right, left))
    rolled, ordered = kernel_call(
        prepare_kernel,
        [FIELD, (SLOTS, PROBE, PROBE)],
        "svv",
        [pltpu.VMEM((2, PROBE, PROBE), BF16)],
        16,
        3 * 10**9,
    )(scalars, probe_field, intensity[0, 0])
    wide, rows = [None] * SLICES, [None] * SLICES
    for k in range(SLICES):
        wide[k], send_a, send_b = kernel_call(widen_kernel, [WIDE, BAND, BAND], "svvv")(
            scalars, own[k], *beside[k]
        )
        rows[k] = swap_rows(send_a, send_b)
    for iteration in range(ITERS):
        last = iteration == ITERS - 1
        (wave,) = kernel_call(
            forward_kernel, [FIELD], "svvvvv", [field] * 2, 20, 3 * 10**9
        )(scalars, wide[0], *rows[0], rolled, space)
        kept1, send_a, send_b, back = kernel_call(
            middle_kernel, [WIDE, BAND, BAND, FIELD], "svvvvvv", [field] * 3, 24, 6 * 10**9
        )(scalars, wide[1], *rows[1], wave, ordered, fourier)
        rows1 = swap_rows(send_a, send_b)
        kept0, send_a, send_b = kernel_call(
            backward_kernel, [WIDE, BAND, BAND], "svvv", [field] * 2, 20, 4 * 10**9
        )(scalars, back, rolled, space)
        rows0 = swap_rows(send_a, send_b)
        kept, back_rows = [kept0, kept1], [rows0, rows1]
        shapes = [CORE, STRIP, STRIP] if last else [WIDE, CORE, CORE]
        fold = fold_last_kernel if last else fold_middle_kernel
        came = [None] * SLICES
        for k in (1, 0):
            total, to_right, to_left = kernel_call(fold, shapes, "svvv")(
                scalars, kept[k], *back_rows[k]
            )
            came[k] = (total, shifted(to_right, "col", 1), shifted(to_left, "col", -1))
        if last:
            (other,) = kernel_call(update_last_kernel, [CORE], "vvvv")(wide[1], *came[1])
            (after,) = kernel_call(finish_kernel, [(CHANNELS, PROBE, PROBE)], "vvvvv")(
                wide[0], *came[0], other
            )
            return after
        for k in (1, 0):
            wide[k], send_a, send_b = kernel_call(
                update_middle_kernel, [WIDE, BAND, BAND], "svvvv"
            )(scalars, wide[k], *came[k])
            rows[k] = swap_rows(send_a, send_b)


def solution(mesh):
    placed = (
        P(None, "row", "col"),
        P(),
        P("row", "col", None, None),
        P("row", "col"),
        P("row", "col", None, None, None),
    )
    return jax.shard_map(
        local, mesh=mesh, in_specs=placed, out_specs=P(None, "row", "col"), check_vma=False
    )
```

time: 184 us -> 136 us (0.74)
  waiting for transfers between devices: 87.2 us -> 57.7 us
  Pallas kernels: 50.6 us -> 30.8 us
  starting transfers between devices: 34.6 us -> 44.6 us
  local copies, waits for them, and re-layouts: 9.54 us -> 1.64 us
    pallas_call x8 -> x17, Pallas kernels: 50.6 us -> 30.8 us  [the longest x2 9.57 us: local(): kernel_call(middle_kernel, [WIDE, BAND, BAND, FIELD], 'svvvvvv', [field]...]
    ppermute x8 -> x16, waiting for transfers between devices: 47.1 us -> 29 us  [swapped(): return lax.ppermute(value, axis, pairs)]
    ppermute x6 -> x12, starting transfers between devices: 13.5 us -> 25.8 us  [shifted(): lax.ppermute(value, axis, [(i, (i + steps) % count) for i in range(count)])]
    ppermute x6 -> x12, waiting for transfers between devices: 40.1 us -> 28.7 us  [shifted(): lax.ppermute(value, axis, [(i, (i + steps) % count) for i in range(count)])]
    unnamed x31 -> x13, local copies, waits for them, and re-layouts: 8.17 us -> 0.12 us
    ppermute x8 -> x16, starting transfers between devices: 21.1 us -> 18.9 us  [swapped(): return lax.ppermute(value, axis, pairs)]
  transfers between devices with their start and end apart: 14 -> 28, of which waited for: 7 -> 13; matrix products, arithmetic and copies ran while one was open for 0% -> 0% of each run, Pallas kernels for 2% -> 13%
where the time goes in v1:
time: 136 us
  waiting for transfers between devices  57.7 us (42%)
  starting transfers between devices  44.6 us (33%)
  Pallas kernels  30.8 us (23%)
  local copies, waits for them, and re-layouts  1.64 us (1%)
    ppermute x16, waiting for transfers between devices, swapped(): return lax.ppermute(value, axis, pairs)  29 us
    ppermute x12, waiting for transfers between devices, shifted(): lax.ppermute(value, axis, [(i, (i + steps) % count) for i in range(count)])  28.7 us
    ppermute x12, starting transfers between devices, shifted(): lax.ppermute(value, axis, [(i, (i + steps) % count) for i in range(count)])  25.8 us
    ppermute x16, starting transfers between devices, swapped(): return lax.ppermute(value, axis, pairs)  18.9 us
    pallas_call x2, Pallas kernels, local(): kernel_call(middle_kernel, [WIDE, BAND, BAND, FIELD], 'svvvvvv', [field]...  9.57 us
    pallas_call x2, Pallas kernels, local(): kernel_call(backward_kernel, [WIDE, BAND, BAND], 'svvv', [field] * 2, 20,...  5.81 us
    pallas_call x2, Pallas kernels, local(): kernel_call(forward_kernel, [FIELD], 'svvvvv', [field] * 2, 20, 3 * 10 ** 9)  5.09 us
    pallas_call x1, Pallas kernels, local(): kernel_call(prepare_kernel, [FIELD, (SLOTS, PROBE, PROBE)], 'svv', [pltpu...  3.34 us
  transfers between devices with their start and end apart: 28, of which 13 were waited for; matrix products, arithmetic and copies ran while one was open for 0% of the time, Pallas kernels for 13%

profile of v1, /device:TPU:0, one launch (start us, length us, event | category | flops | bytes accessed | tf_op | source)
XLA Modules:
  0.0 135.7 jit_solution(4821437593503308077)
XLA Ops:
  0.0 1.4 %fusion = (f32[2,256,128]{2,1,0:T(8,128)S(1)}, f32[2,256,128]{2,1,0:T(8,128)S(1)}, f32[2,256,128]{2,1,0:T(8,128)S(1)}, f32[2,256,128]{2,1,0:T(8,128)S(1)}) fusion(f32[4,256,256]{2,1,0:T(8,128)} %param.7), kind=kLoop, calls=%fused_computation.1 | loop fusion | bytes 2097152 | tf_op jit(solution)/shard_map/slice | solution.py:381
  1.4 2.1 %collective-permute-start.3 = (f32[2,256,128]{2,1,0:T(8,128)S(1)}, f32[2,256,128]{2,1,0:T(8,128)S(1)}, u32[]{:S(2)}, u32[]{:S(2)}) collective-permute-start(f32[2,256,128]{2,1,0:T(8,128)S(1)} %get-tuple-element.85), channel_id=1, source_target_pairs={{0,1},{1,2},{2,3},{3,4},{4,5},{5,6},{6,7},{7,0},{8,9},{9,10},{10,1... | collective-permute-start | bytes 786440 | tf_op jit(solution)/shard_map/ppermute | solution.py:352
  3.5 1.9 %collective-permute-start.1 = (f32[2,256,128]{2,1,0:T(8,128)S(1)}, f32[2,256,128]{2,1,0:T(8,128)S(1)}, u32[]{:S(2)}, u32[]{:S(2)}) collective-permute-start(f32[2,256,128]{2,1,0:T(8,128)S(1)} %get-tuple-element.86), channel_id=1, source_target_pairs={{0,1},{1,2},{2,3},{3,4},{4,5},{5,6},{6,7},{7,0},{8,9},{9,10},{10,1... | collective-permute-start | bytes 786440 | tf_op jit(solution)/shard_map/ppermute | solution.py:352
  5.4 2.2 %collective-permute-start = (f32[2,256,128]{2,1,0:T(8,128)S(1)}, f32[2,256,128]{2,1,0:T(8,128)S(1)}, u32[]{:S(2)}, u32[]{:S(2)}) collective-permute-start(f32[2,256,128]{2,1,0:T(8,128)S(1)} %get-tuple-element.87), channel_id=1, source_target_pairs={{0,7},{1,0},{2,1},{3,2},{4,3},{5,4},{6,5},{7,6},{8,15},{9,8},{10,9... | collective-permute-start | bytes 786440 | tf_op jit(solution)/shard_map/ppermute | solution.py:352
  9.7 8.8 %collective-permute-done.1.left = f32[2,256,128]{2,1,0:T(8,128)S(1)} collective-permute-done((f32[2,256,128]{2,1,0:T(8,128)S(1)}, f32[2,256,128]{2,1,0:T(8,128)S(1)}, u32[]{:S(2)}, u32[]{:S(2)}) %collective-permute-start.1) | collective-permute-done | bytes 262176 | tf_op jit(solution)/shard_map/ppermute | solution.py:352
  19.3 5.3 %collective-permute-start.7 = (f32[2,128,512]{2,1,0:T(8,128)S(1)}, f32[2,128,512]{2,1,0:T(8,128)S(1)}, u32[]{:S(2)}, u32[]{:S(2)}) collective-permute-start(f32[2,128,512]{2,1,0:T(8,128)S(1)} %get-tuple-element.50), channel_id=1, source_target_pairs={{8,16},{16,8},{24,32},{32,24},{40,48},{48,40},{56,64},{64,56},{72,... | collective-permute-start | bytes 1572872 | tf_op jit(solution)/shard_map/ppermute | solution.py:361
  26.2 3.3 %shard_map.75 = (f32[3,2,256,256]{3,2,1,0:T(8,128)S(1)}, f32[3,256,256]{2,1,0:T(8,128)S(1)}) custom-call(s32[8]{0:T(128)S(1)} %pad_add_fusion.offs, f32[2,256,256]{2,1,0:T(8,128)S(1)} %copy-done.1, f32[3,256,256]{2,1,0:T(8,128)S(1)} %bitcast.4), custom_call_target="tpu_custom_call" | custom-call | flops 3000000000 | bytes 1000000 | tf_op jit(solution)/shard_map/pallas_call | solution.py:383
  29.6 2.0 %collective-permute-done.7.row_b = f32[2,128,512]{2,1,0:T(8,128)S(1)} collective-permute-done((f32[2,128,512]{2,1,0:T(8,128)S(1)}, f32[2,128,512]{2,1,0:T(8,128)S(1)}, u32[]{:S(2)}, u32[]{:S(2)}) %collective-permute-start.7) | collective-permute-done | bytes 524320 | tf_op jit(solution)/shard_map/ppermute | solution.py:361
  31.6 2.5 %shard_map.76.wave = f32[3,2,256,256]{3,2,1,0:T(8,128)S(1)} custom-call(s32[8]{0:T(128)S(1)} %pad_add_fusion.offs, f32[2,256,512]{2,1,0:T(8,128)S(1)} %get-tuple-element.45.wide, f32[2,128,512]{2,1,0:T(8,128)S(1)} %collective-permute-done.6.row_a, f32[2,128,512]{2,1,0:T(8,128)S(1)} %collective-permute-done.7.row_b, ...), custom_call_target="tpu_custom_call" | custom-call | flops 3000000000 | bytes 1000000 | tf_op jit(solution)/shard_map/pallas_call | solution.py:399
  34.1 3.5 %collective-permute-done.5.row_b = f32[2,128,512]{2,1,0:T(8,128)S(1)} collective-permute-done((f32[2,128,512]{2,1,0:T(8,128)S(1)}, f32[2,128,512]{2,1,0:T(8,128)S(1)}, u32[]{:S(2)}, u32[]{:S(2)}) %collective-permute-start.5) | collective-permute-done | bytes 524320 | tf_op jit(solution)/shard_map/ppermute | solution.py:361
  37.7 4.8 %shard_map.77 = (f32[2,256,512]{2,1,0:T(8,128)S(1)}, f32[2,128,512]{2,1,0:T(8,128)S(1)}, f32[2,128,512]{2,1,0:T(8,128)S(1)}, f32[3,2,256,256]{3,2,1,0:T(8,128)S(1)}) custom-call(s32[8]{0:T(128)S(1)} %pad_add_fusion.offs, f32[2,256,512]{2,1,0:T(8,128)S(1)} %get-tuple-element.46.wide, f32[2,128,512]{2,1,0:T(8,128)S(1)} %collective-permute-done.4.row_a, ...), custom_call_target="tpu_custom_call" | custom-call | flops 6000000000 | bytes 1000000 | tf_op jit(solution)/shard_map/pallas_call | solution.py:402
  42.4 2.9 %shard_map.78 = (f32[2,256,512]{2,1,0:T(8,128)S(1)}, f32[2,128,512]{2,1,0:T(8,128)S(1)}, f32[2,128,512]{2,1,0:T(8,128)S(1)}) custom-call(s32[8]{0:T(128)S(1)} %pad_add_fusion.offs, f32[3,2,256,256]{3,2,1,0:T(8,128)S(1)} %get-tuple-element.53.back, f32[3,2,256,256]{3,2,1,0:T(8,128)S(1)} %get-tuple-element.51.rolled, bf16[8,256,256]{2,1,0:T(8,128)(2,1)S(1)} %copy-done.2), custom_call_target="tpu_custom_call" | custom-call | flops 4000000000 | bytes 1000000 | tf_op jit(solution)/shard_map/pallas_call | solution.py:406
  45.5 4.8 %collective-permute-start.9 = (f32[2,128,512]{2,1,0:T(8,128)S(1)}, f32[2,128,512]{2,1,0:T(8,128)S(1)}, u32[]{:S(2)}, u32[]{:S(2)}) collective-permute-start(f32[2,128,512]{2,1,0:T(8,128)S(1)} %get-tuple-element.56), channel_id=1, source_target_pairs={{8,16},{16,8},{24,32},{32,24},{40,48},{48,40},{56,64},{64,56},{72,... | collective-permute-start | bytes 1572872 | tf_op jit(solution)/shard_map/ppermute | solution.py:361
  50.9 6.9 %collective-permute-done.9.row_b = f32[2,128,512]{2,1,0:T(8,128)S(1)} collective-permute-done((f32[2,128,512]{2,1,0:T(8,128)S(1)}, f32[2,128,512]{2,1,0:T(8,128)S(1)}, u32[]{:S(2)}, u32[]{:S(2)}) %collective-permute-start.9) | collective-permute-done | bytes 524320 | tf_op jit(solution)/shard_map/ppermute | solution.py:361
  58.6 4.1 %collective-permute-start.11 = (f32[2,256,256]{2,1,0:T(8,128)S(1)}, f32[2,256,256]{2,1,0:T(8,128)S(1)}, u32[]{:S(2)}, u32[]{:S(2)}) collective-permute-start(f32[2,256,256]{2,1,0:T(8,128)S(1)} %get-tuple-element.59), channel_id=1, source_target_pairs={{0,7},{1,0},{2,1},{3,2},{4,3},{5,4},{6,5},{7,6},{8,15},{9,8},{10,9... | collective-permute-start | bytes 1572872 | tf_op jit(solution)/shard_map/ppermute | solution.py:352
  62.7 2.9 %collective-permute-done.13.row_b = f32[2,128,512]{2,1,0:T(8,128)S(1)} collective-permute-done((f32[2,128,512]{2,1,0:T(8,128)S(1)}, f32[2,128,512]{2,1,0:T(8,128)S(1)}, u32[]{:S(2)}, u32[]{:S(2)}) %collective-permute-start.13) | collective-permute-done | bytes 524320 | tf_op jit(solution)/shard_map/ppermute | solution.py:361
  66.4 4.1 %collective-permute-start.15 = (f32[2,256,256]{2,1,0:T(8,128)S(1)}, f32[2,256,256]{2,1,0:T(8,128)S(1)}, u32[]{:S(2)}, u32[]{:S(2)}) collective-permute-start(f32[2,256,256]{2,1,0:T(8,128)S(1)} %get-tuple-element.66), channel_id=1, source_target_pairs={{0,7},{1,0},{2,1},{3,2},{4,3},{5,4},{6,5},{7,6},{8,15},{9,8},{10,9... | collective-permute-start | bytes 1572872 | tf_op jit(solution)/shard_map/ppermute | solution.py:352
  70.5 8.7 %collective-permute-done.10.from_left = f32[2,256,256]{2,1,0:T(8,128)S(1)} collective-permute-done((f32[2,256,256]{2,1,0:T(8,128)S(1)}, f32[2,256,256]{2,1,0:T(8,128)S(1)}, u32[]{:S(2)}, u32[]{:S(2)}) %collective-permute-start.10) | collective-permute-done | bytes 524320 | tf_op jit(solution)/shard_map/ppermute | solution.py:352
  80.3 6.4 %collective-permute-done.14.from_left = f32[2,256,256]{2,1,0:T(8,128)S(1)} collective-permute-done((f32[2,256,256]{2,1,0:T(8,128)S(1)}, f32[2,256,256]{2,1,0:T(8,128)S(1)}, u32[]{:S(2)}, u32[]{:S(2)}) %collective-permute-start.14) | collective-permute-done | bytes 524320 | tf_op jit(solution)/shard_map/ppermute | solution.py:352
  88.5 5.2 %collective-permute-done.19.row_b = f32[2,128,512]{2,1,0:T(8,128)S(1)} collective-permute-done((f32[2,128,512]{2,1,0:T(8,128)S(1)}, f32[2,128,512]{2,1,0:T(8,128)S(1)}, u32[]{:S(2)}, u32[]{:S(2)}) %collective-permute-start.19) | collective-permute-done | bytes 524320 | tf_op jit(solution)/shard_map/ppermute | solution.py:361
  93.7 2.5 %shard_map.83.wave = f32[3,2,256,256]{3,2,1,0:T(8,128)S(1)} custom-call(s32[8]{0:T(128)S(1)} %pad_add_fusion.offs, f32[2,256,512]{2,1,0:T(8,128)S(1)} %get-tuple-element.60.wide, f32[2,128,512]{2,1,0:T(8,128)S(1)} %collective-permute-done.18.row_a, f32[2,128,512]{2,1,0:T(8,128)S(1)} %collective-permute-done.19.row_b, ...), custom_call_target="tpu_custom_call" | custom-call | flops 3000000000 | bytes 1000000 | tf_op jit(solution)/shard_map/pallas_call | solution.py:399
  96.3 3.5 %collective-permute-done.17.row_b = f32[2,128,512]{2,1,0:T(8,128)S(1)} collective-permute-done((f32[2,128,512]{2,1,0:T(8,128)S(1)}, f32[2,128,512]{2,1,0:T(8,128)S(1)}, u32[]{:S(2)}, u32[]{:S(2)}) %collective-permute-start.17) | collective-permute-done | bytes 524320 | tf_op jit(solution)/shard_map/ppermute | solution.py:361
  99.8 4.8 %shard_map.84 = (f32[2,256,512]{2,1,0:T(8,128)S(1)}, f32[2,128,512]{2,1,0:T(8,128)S(1)}, f32[2,128,512]{2,1,0:T(8,128)S(1)}, f32[3,2,256,256]{3,2,1,0:T(8,128)S(1)}) custom-call(s32[8]{0:T(128)S(1)} %pad_add_fusion.offs, f32[2,256,512]{2,1,0:T(8,128)S(1)} %get-tuple-element.67.wide, f32[2,128,512]{2,1,0:T(8,128)S(1)} %collective-permute-done.16.row_a, ...), custom_call_target="tpu_custom_call" | custom-call | flops 6000000000 | bytes 1000000 | tf_op jit(solution)/shard_map/pallas_call | solution.py:402
  104.7 2.1 %collective-permute-start.25 = (f32[2,128,512]{2,1,0:T(8,128)S(1)}, f32[2,128,512]{2,1,0:T(8,128)S(1)}, u32[]{:S(2)}, u32[]{:S(2)}) collective-permute-start(f32[2,128,512]{2,1,0:T(8,128)S(1)} %get-tuple-element.81), channel_id=1, source_target_pairs={{8,16},{16,8},{24,32},{32,24},{40,48},{48,40},{56,64},{64,56},{72,... | collective-permute-start | bytes 1572872 | tf_op jit(solution)/shard_map/ppermute | solution.py:361
  106.8 2.9 %shard_map.85 = (f32[2,256,512]{2,1,0:T(8,128)S(1)}, f32[2,128,512]{2,1,0:T(8,128)S(1)}, f32[2,128,512]{2,1,0:T(8,128)S(1)}) custom-call(s32[8]{0:T(128)S(1)} %pad_add_fusion.offs, f32[3,2,256,256]{3,2,1,0:T(8,128)S(1)} %get-tuple-element.72.back, f32[3,2,256,256]{3,2,1,0:T(8,128)S(1)} %get-tuple-element.51.rolled, bf16[8,256,256]{2,1,0:T(8,128)(2,1)S(1)} %copy-done.2), custom_call_target="tpu_custom_call" | custom-call | flops 4000000000 | bytes 1000000 | tf_op jit(solution)/shard_map/pallas_call | solution.py:406
  109.8 3.4 %collective-permute-start.21 = (f32[2,128,512]{2,1,0:T(8,128)S(1)}, f32[2,128,512]{2,1,0:T(8,128)S(1)}, u32[]{:S(2)}, u32[]{:S(2)}) collective-permute-start(f32[2,128,512]{2,1,0:T(8,128)S(1)} %get-tuple-element.75), channel_id=1, source_target_pairs={{8,16},{16,8},{24,32},{32,24},{40,48},{48,40},{56,64},{64,56},{72,... | collective-permute-start | bytes 1572872 | tf_op jit(solution)/shard_map/ppermute | solution.py:361
  113.2 3.8 %collective-permute-done.25.row_b = f32[2,128,512]{2,1,0:T(8,128)S(1)} collective-permute-done((f32[2,128,512]{2,1,0:T(8,128)S(1)}, f32[2,128,512]{2,1,0:T(8,128)S(1)}, u32[]{:S(2)}, u32[]{:S(2)}) %collective-permute-start.25) | collective-permute-done | bytes 524320 | tf_op jit(solution)/shard_map/ppermute | solution.py:361
  117.8 4.1 %collective-permute-start.27 = (f32[2,256,128]{2,1,0:T(8,128)S(1)}, f32[2,256,128]{2,1,0:T(8,128)S(1)}, u32[]{:S(2)}, u32[]{:S(2)}) collective-permute-start(f32[2,256,128]{2,1,0:T(8,128)S(1)} %get-tuple-element.84), channel_id=1, source_target_pairs={{0,7},{1,0},{2,1},{3,2},{4,3},{5,4},{6,5},{7,6},{8,15},{9,8},{10,9... | collective-permute-start | bytes 786440 | tf_op jit(solution)/shard_map/ppermute | solution.py:352
  121.9 1.2 collective-permute-done.21.row_b
  123.9 5.9 %collective-permute-start.23 = (f32[2,256,128]{2,1,0:T(8,128)S(1)}, f32[2,256,128]{2,1,0:T(8,128)S(1)}, u32[]{:S(2)}, u32[]{:S(2)}) collective-permute-start(f32[2,256,128]{2,1,0:T(8,128)S(1)} %get-tuple-element.78), channel_id=1, source_target_pairs={{0,7},{1,0},{2,1},{3,2},{4,3},{5,4},{6,5},{7,6},{8,15},{9,8},{10,9... | collective-permute-start | bytes 786440 | tf_op jit(solution)/shard_map/ppermute | solution.py:352
  129.7 2.1 %collective-permute-done.26.from_left = f32[2,256,128]{2,1,0:T(8,128)S(1)} collective-permute-done((f32[2,256,128]{2,1,0:T(8,128)S(1)}, f32[2,256,128]{2,1,0:T(8,128)S(1)}, u32[]{:S(2)}, u32[]{:S(2)}) %collective-permute-start.26) | collective-permute-done | bytes 262176 | tf_op jit(solution)/shard_map/ppermute | solution.py:352
  131.9 2.7 %collective-permute-done.22.from_left = f32[2,256,128]{2,1,0:T(8,128)S(1)} collective-permute-done((f32[2,256,128]{2,1,0:T(8,128)S(1)}, f32[2,256,128]{2,1,0:T(8,128)S(1)}, u32[]{:S(2)}, u32[]{:S(2)}) %collective-permute-start.22) | collective-permute-done | bytes 262176 | tf_op jit(solution)/shard_map/ppermute | solution.py:352
  (58 shorter events, 11.9 us)
Async XLA Ops:
  0.0 9.5 %copy-start.4 = (f32[4,256,256]{2,1,0:T(8,128)S(1)}, f32[4,256,256]{2,1,0:T(8,128)}, u32[]{:S(2)}) copy-start(f32[4,256,256]{2,1,0:T(8,128)} %param.7) | copy-start | bytes 3145732
  0.0 9.3 %copy-start.5 = (s32[1,1,3,2]{2,3,1,0:T(2,128)S(1)}, s32[1,1,3,2]{2,3,1,0:T(2,128)}, u32[]{:S(2)}) copy-start(s32[1,1,3,2]{2,3,1,0:T(2,128)} %param.9) | copy-start | bytes 76
  1.4 23.2 %collective-permute-start.3 = (f32[2,256,128]{2,1,0:T(8,128)S(1)}, f32[2,256,128]{2,1,0:T(8,128)S(1)}, u32[]{:S(2)}, u32[]{:S(2)}) collective-permute-start(f32[2,256,128]{2,1,0:T(8,128)S(1)} %get-tuple-element.85), channel_id=1, source_target_pairs={{0,1},{1,2},{2,3},{3,4},{4,5},{5,6},{6,7},{7,0},{8,9},{9,10},{10,1... | collective-permute-start | bytes 786440 | tf_op jit(solution)/shard_map/ppermute | solution.py:352
  3.5 15.0 %collective-permute-start.1 = (f32[2,256,128]{2,1,0:T(8,128)S(1)}, f32[2,256,128]{2,1,0:T(8,128)S(1)}, u32[]{:S(2)}, u32[]{:S(2)}) collective-permute-start(f32[2,256,128]{2,1,0:T(8,128)S(1)} %get-tuple-element.86), channel_id=1, source_target_pairs={{0,1},{1,2},{2,3},{3,4},{4,5},{5,6},{6,7},{7,0},{8,9},{9,10},{10,1... | collective-permute-start | bytes 786440 | tf_op jit(solution)/shard_map/ppermute | solution.py:352
  5.4 13.1 %collective-permute-start = (f32[2,256,128]{2,1,0:T(8,128)S(1)}, f32[2,256,128]{2,1,0:T(8,128)S(1)}, u32[]{:S(2)}, u32[]{:S(2)}) collective-permute-start(f32[2,256,128]{2,1,0:T(8,128)S(1)} %get-tuple-element.87), channel_id=1, source_target_pairs={{0,7},{1,0},{2,1},{3,2},{4,3},{5,4},{6,5},{7,6},{8,15},{9,8},{10,9... | collective-permute-start | bytes 786440 | tf_op jit(solution)/shard_map/ppermute | solution.py:352
  7.6 16.9 %collective-permute-start.2 = (f32[2,256,128]{2,1,0:T(8,128)S(1)}, f32[2,256,128]{2,1,0:T(8,128)S(1)}, u32[]{:S(2)}, u32[]{:S(2)}) collective-permute-start(f32[2,256,128]{2,1,0:T(8,128)S(1)} %get-tuple-element.88), channel_id=1, source_target_pairs={{0,7},{1,0},{2,1},{3,2},{4,3},{5,4},{6,5},{7,6},{8,15},{9,8},{10,9... | collective-permute-start | bytes 786440 | tf_op jit(solution)/shard_map/ppermute | solution.py:352
  9.6 16.6 %copy-start = (f32[1,1,3,256,256]{4,3,2,1,0:T(8,128)S(1)}, f32[1,1,3,256,256]{4,3,2,1,0:T(8,128)}, u32[]{:S(2)}) copy-start(f32[1,1,3,256,256]{4,3,2,1,0:T(8,128)} %param.11) | copy-start | bytes 2359300
  9.6 16.6 %copy-start.1 = (f32[2,256,256]{2,1,0:T(8,128)S(1)}, f32[2,256,256]{2,1,0:T(8,128)}, u32[]{:S(2)}) copy-start(f32[2,256,256]{2,1,0:T(8,128)} %probe.1) | copy-start | bytes 1572868
  19.2 10.4 %collective-permute-start.6 = (f32[2,128,512]{2,1,0:T(8,128)S(1)}, f32[2,128,512]{2,1,0:T(8,128)S(1)}, u32[]{:S(2)}, u32[]{:S(2)}) collective-permute-start(f32[2,128,512]{2,1,0:T(8,128)S(1)} %get-tuple-element.49), channel_id=1, source_target_pairs={{0,8},{8,0},{16,24},{24,16},{32,40},{40,32},{48,56},{56,48},{64,72... | collective-permute-start | bytes 1572872 | tf_op jit(solution)/shard_map/ppermute | solution.py:361
  19.3 12.3 %collective-permute-start.7 = (f32[2,128,512]{2,1,0:T(8,128)S(1)}, f32[2,128,512]{2,1,0:T(8,128)S(1)}, u32[]{:S(2)}, u32[]{:S(2)}) collective-permute-start(f32[2,128,512]{2,1,0:T(8,128)S(1)} %get-tuple-element.50), channel_id=1, source_target_pairs={{8,16},{16,8},{24,32},{32,24},{40,48},{48,40},{56,64},{64,56},{72,... | collective-permute-start | bytes 1572872 | tf_op jit(solution)/shard_map/ppermute | solution.py:361
  25.3 8.9 %collective-permute-start.4 = (f32[2,128,512]{2,1,0:T(8,128)S(1)}, f32[2,128,512]{2,1,0:T(8,128)S(1)}, u32[]{:S(2)}, u32[]{:S(2)}) collective-permute-start(f32[2,128,512]{2,1,0:T(8,128)S(1)} %get-tuple-element.47), channel_id=1, source_target_pairs={{0,8},{8,0},{16,24},{24,16},{32,40},{40,32},{48,56},{56,48},{64,72... | collective-permute-start | bytes 1572872 | tf_op jit(solution)/shard_map/ppermute | solution.py:361
  25.3 12.3 %collective-permute-start.5 = (f32[2,128,512]{2,1,0:T(8,128)S(1)}, f32[2,128,512]{2,1,0:T(8,128)S(1)}, u32[]{:S(2)}, u32[]{:S(2)}) collective-permute-start(f32[2,128,512]{2,1,0:T(8,128)S(1)} %get-tuple-element.48), channel_id=1, source_target_pairs={{8,16},{16,8},{24,32},{32,24},{40,48},{48,40},{56,64},{64,56},{72,... | collective-permute-start | bytes 1572872 | tf_op jit(solution)/shard_map/ppermute | solution.py:361
  45.4 5.5 %collective-permute-start.8 = (f32[2,128,512]{2,1,0:T(8,128)S(1)}, f32[2,128,512]{2,1,0:T(8,128)S(1)}, u32[]{:S(2)}, u32[]{:S(2)}) collective-permute-start(f32[2,128,512]{2,1,0:T(8,128)S(1)} %get-tuple-element.55), channel_id=1, source_target_pairs={{0,8},{8,0},{16,24},{24,16},{32,40},{40,32},{48,56},{56,48},{64,72... | collective-permute-start | bytes 1572872 | tf_op jit(solution)/shard_map/ppermute | solution.py:361
  45.5 12.3 %collective-permute-start.9 = (f32[2,128,512]{2,1,0:T(8,128)S(1)}, f32[2,128,512]{2,1,0:T(8,128)S(1)}, u32[]{:S(2)}, u32[]{:S(2)}) collective-permute-start(f32[2,128,512]{2,1,0:T(8,128)S(1)} %get-tuple-element.56), channel_id=1, source_target_pairs={{8,16},{16,8},{24,32},{32,24},{40,48},{48,40},{56,64},{64,56},{72,... | collective-permute-start | bytes 1572872 | tf_op jit(solution)/shard_map/ppermute | solution.py:361
  50.3 12.4 %collective-permute-start.12 = (f32[2,128,512]{2,1,0:T(8,128)S(1)}, f32[2,128,512]{2,1,0:T(8,128)S(1)}, u32[]{:S(2)}, u32[]{:S(2)}) collective-permute-start(f32[2,128,512]{2,1,0:T(8,128)S(1)} %get-tuple-element.62), channel_id=1, source_target_pairs={{0,8},{8,0},{16,24},{24,16},{32,40},{40,32},{48,56},{56,48},{64,72... | collective-permute-start | bytes 1572872 | tf_op jit(solution)/shard_map/ppermute | solution.py:361
  50.3 15.3 %collective-permute-start.13 = (f32[2,128,512]{2,1,0:T(8,128)S(1)}, f32[2,128,512]{2,1,0:T(8,128)S(1)}, u32[]{:S(2)}, u32[]{:S(2)}) collective-permute-start(f32[2,128,512]{2,1,0:T(8,128)S(1)} %get-tuple-element.63), channel_id=1, source_target_pairs={{8,16},{16,8},{24,32},{32,24},{40,48},{48,40},{56,64},{64,56},{72,... | collective-permute-start | bytes 1572872 | tf_op jit(solution)/shard_map/ppermute | solution.py:361
  58.5 20.7 %collective-permute-start.10 = (f32[2,256,256]{2,1,0:T(8,128)S(1)}, f32[2,256,256]{2,1,0:T(8,128)S(1)}, u32[]{:S(2)}, u32[]{:S(2)}) collective-permute-start(f32[2,256,256]{2,1,0:T(8,128)S(1)} %get-tuple-element.58), channel_id=1, source_target_pairs={{0,1},{1,2},{2,3},{3,4},{4,5},{5,6},{6,7},{7,0},{8,9},{9,10},{10,1... | collective-permute-start | bytes 1572872 | tf_op jit(solution)/shard_map/ppermute | solution.py:352
  58.6 20.7 %collective-permute-start.11 = (f32[2,256,256]{2,1,0:T(8,128)S(1)}, f32[2,256,256]{2,1,0:T(8,128)S(1)}, u32[]{:S(2)}, u32[]{:S(2)}) collective-permute-start(f32[2,256,256]{2,1,0:T(8,128)S(1)} %get-tuple-element.59), channel_id=1, source_target_pairs={{0,7},{1,0},{2,1},{3,2},{4,3},{5,4},{6,5},{7,6},{8,15},{9,8},{10,9... | collective-permute-start | bytes 1572872 | tf_op jit(solution)/shard_map/ppermute | solution.py:352
  66.3 20.4 %collective-permute-start.14 = (f32[2,256,256]{2,1,0:T(8,128)S(1)}, f32[2,256,256]{2,1,0:T(8,128)S(1)}, u32[]{:S(2)}, u32[]{:S(2)}) collective-permute-start(f32[2,256,256]{2,1,0:T(8,128)S(1)} %get-tuple-element.65), channel_id=1, source_target_pairs={{0,1},{1,2},{2,3},{3,4},{4,5},{5,6},{6,7},{7,0},{8,9},{9,10},{10,1... | collective-permute-start | bytes 1572872 | tf_op jit(solution)/shard_map/ppermute | solution.py:352
  66.4 20.3 %collective-permute-start.15 = (f32[2,256,256]{2,1,0:T(8,128)S(1)}, f32[2,256,256]{2,1,0:T(8,128)S(1)}, u32[]{:S(2)}, u32[]{:S(2)}) collective-permute-start(f32[2,256,256]{2,1,0:T(8,128)S(1)} %get-tuple-element.66), channel_id=1, source_target_pairs={{0,7},{1,0},{2,1},{3,2},{4,3},{5,4},{6,5},{7,6},{8,15},{9,8},{10,9... | collective-permute-start | bytes 1572872 | tf_op jit(solution)/shard_map/ppermute | solution.py:352
  80.0 8.5 %collective-permute-start.18 = (f32[2,128,512]{2,1,0:T(8,128)S(1)}, f32[2,128,512]{2,1,0:T(8,128)S(1)}, u32[]{:S(2)}, u32[]{:S(2)}) collective-permute-start(f32[2,128,512]{2,1,0:T(8,128)S(1)} %get-tuple-element.70), channel_id=1, source_target_pairs={{0,8},{8,0},{16,24},{24,16},{32,40},{40,32},{48,56},{56,48},{64,72... | collective-permute-start | bytes 1572872 | tf_op jit(solution)/shard_map/ppermute | solution.py:361
  80.1 13.6 %collective-permute-start.19 = (f32[2,128,512]{2,1,0:T(8,128)S(1)}, f32[2,128,512]{2,1,0:T(8,128)S(1)}, u32[]{:S(2)}, u32[]{:S(2)}) collective-permute-start(f32[2,128,512]{2,1,0:T(8,128)S(1)} %get-tuple-element.71), channel_id=1, source_target_pairs={{8,16},{16,8},{24,32},{32,24},{40,48},{48,40},{56,64},{64,56},{72,... | collective-permute-start | bytes 1572872 | tf_op jit(solution)/shard_map/ppermute | solution.py:361
  87.4 8.9 %collective-permute-start.16 = (f32[2,128,512]{2,1,0:T(8,128)S(1)}, f32[2,128,512]{2,1,0:T(8,128)S(1)}, u32[]{:S(2)}, u32[]{:S(2)}) collective-permute-start(f32[2,128,512]{2,1,0:T(8,128)S(1)} %get-tuple-element.68), channel_id=1, source_target_pairs={{0,8},{8,0},{16,24},{24,16},{32,40},{40,32},{48,56},{56,48},{64,72... | collective-permute-start | bytes 1572872 | tf_op jit(solution)/shard_map/ppermute | solution.py:361
  87.5 12.3 %collective-permute-start.17 = (f32[2,128,512]{2,1,0:T(8,128)S(1)}, f32[2,128,512]{2,1,0:T(8,128)S(1)}, u32[]{:S(2)}, u32[]{:S(2)}) collective-permute-start(f32[2,128,512]{2,1,0:T(8,128)S(1)} %get-tuple-element.69), channel_id=1, source_target_pairs={{8,16},{16,8},{24,32},{32,24},{40,48},{48,40},{56,64},{64,56},{72,... | collective-permute-start | bytes 1572872 | tf_op jit(solution)/shard_map/ppermute | solution.py:361
  104.6 8.6 %collective-permute-start.24 = (f32[2,128,512]{2,1,0:T(8,128)S(1)}, f32[2,128,512]{2,1,0:T(8,128)S(1)}, u32[]{:S(2)}, u32[]{:S(2)}) collective-permute-start(f32[2,128,512]{2,1,0:T(8,128)S(1)} %get-tuple-element.80), channel_id=1, source_target_pairs={{0,8},{8,0},{16,24},{24,16},{32,40},{40,32},{48,56},{56,48},{64,72... | collective-permute-start | bytes 1572872 | tf_op jit(solution)/shard_map/ppermute | solution.py:361
  104.7 12.3 %collective-permute-start.25 = (f32[2,128,512]{2,1,0:T(8,128)S(1)}, f32[2,128,512]{2,1,0:T(8,128)S(1)}, u32[]{:S(2)}, u32[]{:S(2)}) collective-permute-start(f32[2,128,512]{2,1,0:T(8,128)S(1)} %get-tuple-element.81), channel_id=1, source_target_pairs={{8,16},{16,8},{24,32},{32,24},{40,48},{48,40},{56,64},{64,56},{72,... | collective-permute-start | bytes 1572872 | tf_op jit(solution)/shard_map/ppermute | solution.py:361
  109.7 12.2 %collective-permute-start.20 = (f32[2,128,512]{2,1,0:T(8,128)S(1)}, f32[2,128,512]{2,1,0:T(8,128)S(1)}, u32[]{:S(2)}, u32[]{:S(2)}) collective-permute-start(f32[2,128,512]{2,1,0:T(8,128)S(1)} %get-tuple-element.74), channel_id=1, source_target_pairs={{0,8},{8,0},{16,24},{24,16},{32,40},{40,32},{48,56},{56,48},{64,72... | collective-permute-start | bytes 1572872 | tf_op jit(solution)/shard_map/ppermute | solution.py:361
  109.8 13.3 %collective-permute-start.21 = (f32[2,128,512]{2,1,0:T(8,128)S(1)}, f32[2,128,512]{2,1,0:T(8,128)S(1)}, u32[]{:S(2)}, u32[]{:S(2)}) collective-permute-start(f32[2,128,512]{2,1,0:T(8,128)S(1)} %get-tuple-element.75), channel_id=1, source_target_pairs={{8,16},{16,8},{24,32},{32,24},{40,48},{48,40},{56,64},{64,56},{72,... | collective-permute-start | bytes 1572872 | tf_op jit(solution)/shard_map/ppermute | solution.py:361
  117.7 14.1 %collective-permute-start.26 = (f32[2,256,128]{2,1,0:T(8,128)S(1)}, f32[2,256,128]{2,1,0:T(8,128)S(1)}, u32[]{:S(2)}, u32[]{:S(2)}) collective-permute-start(f32[2,256,128]{2,1,0:T(8,128)S(1)} %get-tuple-element.83), channel_id=1, source_target_pairs={{0,1},{1,2},{2,3},{3,4},{4,5},{5,6},{6,7},{7,0},{8,9},{9,10},{10,1... | collective-permute-start | bytes 786440 | tf_op jit(solution)/shard_map/ppermute | solution.py:352
  117.8 14.0 %collective-permute-start.27 = (f32[2,256,128]{2,1,0:T(8,128)S(1)}, f32[2,256,128]{2,1,0:T(8,128)S(1)}, u32[]{:S(2)}, u32[]{:S(2)}) collective-permute-start(f32[2,256,128]{2,1,0:T(8,128)S(1)} %get-tuple-element.84), channel_id=1, source_target_pairs={{0,7},{1,0},{2,1},{3,2},{4,3},{5,4},{6,5},{7,6},{8,15},{9,8},{10,9... | collective-permute-start | bytes 786440 | tf_op jit(solution)/shard_map/ppermute | solution.py:352
  123.8 10.8 %collective-permute-start.22 = (f32[2,256,128]{2,1,0:T(8,128)S(1)}, f32[2,256,128]{2,1,0:T(8,128)S(1)}, u32[]{:S(2)}, u32[]{:S(2)}) collective-permute-start(f32[2,256,128]{2,1,0:T(8,128)S(1)} %get-tuple-element.77), channel_id=1, source_target_pairs={{0,1},{1,2},{2,3},{3,4},{4,5},{5,6},{6,7},{7,0},{8,9},{9,10},{10,1... | collective-permute-start | bytes 786440 | tf_op jit(solution)/shard_map/ppermute | solution.py:352
  123.9 10.7 %collective-permute-start.23 = (f32[2,256,128]{2,1,0:T(8,128)S(1)}, f32[2,256,128]{2,1,0:T(8,128)S(1)}, u32[]{:S(2)}, u32[]{:S(2)}) collective-permute-start(f32[2,256,128]{2,1,0:T(8,128)S(1)} %get-tuple-element.78), channel_id=1, source_target_pairs={{0,7},{1,0},{2,1},{3,2},{4,3},{5,4},{6,5},{7,6},{8,15},{9,8},{10,9... | collective-permute-start | bytes 786440 | tf_op jit(solution)/shard_map/ppermute | solution.py:352
  (2 other events, 11.5 us)

commit v2 on v1

--- a/solution.py
+++ b/solution.py
@@ -7,6 +7,7 @@
 from jax.experimental import pallas as pl
 from jax.experimental.pallas import tpu as pltpu
 from jax.sharding import PartitionSpec as P
+
 
 PROBE = 256
 HALF = 128
@@ -249,7 +250,7 @@
     spread(offs, work, kept, send_a, send_b)
 
 
-def widen_kernel(offs, own, right, left, wide, send_a, send_b):
+def widen_kernel(first, offs, own, right, left, wide, send_a, send_b):
     for target, half in row_halves(offs, send_a, send_b, False):
 
         @chunks(half)
@@ -257,7 +258,7 @@
             rows = pl.ds(base, CHUNK)
             for part in range(2):
                 for ref, here in ((wide, rows), (target, part_rows)):
-                    ref[part, here, :256] = own[part, rows, :]
+                    ref[part, here, :256] = own[first + part, rows, :]
                     ref[part, here, 256:384] = right[part, rows, :]
                     ref[part, here, 384:] = left[part, rows, :]
 
@@ -366,6 +367,10 @@
     return swapped(send_a, "row", 0), row_b
 
 
+def pass_cols(to_right, to_left):
+    return shifted(to_right, "col", 1), shifted(to_left, "col", -1)
+
+
 def local(object_core, probe_field, offsets, tile_counts, intensity):
     parity = lax.axis_index("row") % 2
     scalars = jnp.concatenate(
@@ -375,11 +380,7 @@
     field = pltpu.VMEM(FIELD, F32)
 
     own = [object_core[2 * k : 2 * k + 2] for k in range(SLICES)]
-    beside = []
-    for cells in own:
-        right = shifted(cells[:, :, :HALF], "col", -1)
-        left = shifted(cells[:, :, HALF:], "col", 1)
-        beside.append((right, left))
+    beside = [pass_cols(cells[:, :, HALF:], cells[:, :, :HALF]) for cells in own]
     rolled, ordered = kernel_call(
         prepare_kernel,
         [FIELD, (SLOTS, PROBE, PROBE)],
@@ -390,9 +391,10 @@
     )(scalars, probe_field, intensity[0, 0])
     wide, rows = [None] * SLICES, [None] * SLICES
     for k in range(SLICES):
-        wide[k], send_a, send_b = kernel_call(widen_kernel, [WIDE, BAND, BAND], "svvv")(
-            scalars, own[k], *beside[k]
-        )
+        left, right = beside[k]
+        wide[k], send_a, send_b = kernel_call(
+            functools.partial(widen_kernel, 2 * k), [WIDE, BAND, BAND], "svvv"
+        )(scalars, object_core, right, left)
         rows[k] = swap_rows(send_a, send_b)
     for iteration in range(ITERS):
         last = iteration == ITERS - 1
@@ -415,7 +417,7 @@
             total, to_right, to_left = kernel_call(fold, shapes, "svvv")(
                 scalars, kept[k], *back_rows[k]
             )
-            came[k] = (total, shifted(to_right, "col", 1), shifted(to_left, "col", -1))
+            came[k] = (total, *pass_cols(to_right, to_left))
         if last:
             (other,) = kernel_call(update_last_kernel, [CORE], "vvvv")(wide[1], *came[1])
             (after,) = kernel_call(finish_kernel, [(CHANNELS, PROBE, PROBE)], "vvvvv")(

time: 136 us -> 133 us (0.978)
  waiting for transfers between devices: 57.7 us -> 49.8 us
  starting transfers between devices: 44.6 us -> 49.6 us
    ppermute x12, waiting for transfers between devices: 28.7 us -> 22.8 us  [shifted(): lax.ppermute(value, axis, [(i, (i + steps) % count) for i in range(count)])]
    ppermute x16, starting transfers between devices: 18.9 us -> 21.9 us  [swapped(): return lax.ppermute(value, axis, pairs)]
    ppermute x16, waiting for transfers between devices: 29 us -> 26.9 us  [swapped(): return lax.ppermute(value, axis, pairs)]
    ppermute x12, starting transfers between devices: 25.8 us -> 27.6 us  [shifted(): lax.ppermute(value, axis, [(i, (i + steps) % count) for i in range(count)])]
  transfers between devices with their start and end apart: 28 -> 28, of which waited for: 13 -> 12; matrix products, arithmetic and copies ran while one was open for 0% -> 0% of each run, Pallas kernels for 13% -> 13%
where the time goes in v2:
time: 133 us
  waiting for transfers between devices  49.8 us (37%)
  starting transfers between devices  49.6 us (37%)
  Pallas kernels  30.8 us (23%)
  local copies, waits for them, and re-layouts  1.56 us (1%)
    ppermute x12, starting transfers between devices, shifted(): lax.ppermute(value, axis, [(i, (i + steps) % count) for i in range(count)])  27.6 us
    ppermute x16, waiting for transfers between devices, swapped(): return lax.ppermute(value, axis, pairs)  26.9 us
    ppermute x12, waiting for transfers between devices, shifted(): lax.ppermute(value, axis, [(i, (i + steps) % count) for i in range(count)])  22.8 us
    ppermute x16, starting transfers between devices, swapped(): return lax.ppermute(value, axis, pairs)  21.9 us
    pallas_call x2, Pallas kernels, local(): kernel_call(middle_kernel, [WIDE, BAND, BAND, FIELD], 'svvvvvv', [field]...  9.57 us
    pallas_call x2, Pallas kernels, local(): kernel_call(backward_kernel, [WIDE, BAND, BAND], 'svvv', [field] * 2, 20,...  5.82 us
    pallas_call x2, Pallas kernels, local(): kernel_call(forward_kernel, [FIELD], 'svvvvv', [field] * 2, 20, 3 * 10 ** 9)  5.09 us
    pallas_call x1, Pallas kernels, local(): kernel_call(prepare_kernel, [FIELD, (SLOTS, PROBE, PROBE)], 'svv', [pltpu...  3.34 us
  transfers between devices with their start and end apart: 28, of which 12 were waited for; matrix products, arithmetic and copies ran while one was open for 0% of the time, Pallas kernels for 13%

profile of v2, /device:TPU:0, one launch (start us, length us, event | category | flops | bytes accessed | tf_op | source)
XLA Modules:
  0.0 132.7 jit_solution(2907151053084673747)
XLA Ops:
  0.0 1.4 %fusion = (f32[2,256,128]{2,1,0:T(8,128)S(1)}, f32[2,256,128]{2,1,0:T(8,128)S(1)}, f32[2,256,128]{2,1,0:T(8,128)S(1)}, f32[2,256,128]{2,1,0:T(8,128)S(1)}) fusion(f32[4,256,256]{2,1,0:T(8,128)} %own.3), kind=kLoop, calls=%fused_computation.1 | loop fusion | bytes 2097152 | tf_op jit(solution)/shard_map/slice | solution.py:383
  1.4 2.1 %collective-permute-start.1 = (f32[2,256,128]{2,1,0:T(8,128)S(1)}, f32[2,256,128]{2,1,0:T(8,128)S(1)}, u32[]{:S(2)}, u32[]{:S(2)}) collective-permute-start(f32[2,256,128]{2,1,0:T(8,128)S(1)} %get-tuple-element.87), channel_id=1, source_target_pairs={{0,1},{1,2},{2,3},{3,4},{4,5},{5,6},{6,7},{7,0},{8,9},{9,10},{10,1... | collective-permute-start | bytes 786440 | tf_op jit(solution)/shard_map/ppermute | solution.py:353
  3.5 3.1 %collective-permute-start = (f32[2,256,128]{2,1,0:T(8,128)S(1)}, f32[2,256,128]{2,1,0:T(8,128)S(1)}, u32[]{:S(2)}, u32[]{:S(2)}) collective-permute-start(f32[2,256,128]{2,1,0:T(8,128)S(1)} %get-tuple-element.88), channel_id=1, source_target_pairs={{0,7},{1,0},{2,1},{3,2},{4,3},{5,4},{6,5},{7,6},{8,15},{9,8},{10,9... | collective-permute-start | bytes 786440 | tf_op jit(solution)/shard_map/ppermute | solution.py:353
  6.6 4.1 %collective-permute-start.2 = (f32[2,256,128]{2,1,0:T(8,128)S(1)}, f32[2,256,128]{2,1,0:T(8,128)S(1)}, u32[]{:S(2)}, u32[]{:S(2)}) collective-permute-start(f32[2,256,128]{2,1,0:T(8,128)S(1)} %get-tuple-element.86), channel_id=1, source_target_pairs={{0,7},{1,0},{2,1},{3,2},{4,3},{5,4},{6,5},{7,6},{8,15},{9,8},{10,9... | collective-permute-start | bytes 786440 | tf_op jit(solution)/shard_map/ppermute | solution.py:353
  11.7 2.0 %collective-permute-done.1.left = f32[2,256,128]{2,1,0:T(8,128)S(1)} collective-permute-done((f32[2,256,128]{2,1,0:T(8,128)S(1)}, f32[2,256,128]{2,1,0:T(8,128)S(1)}, u32[]{:S(2)}, u32[]{:S(2)}) %collective-permute-start.1) | collective-permute-done | bytes 262176 | tf_op jit(solution)/shard_map/ppermute | solution.py:353
  14.5 5.3 %collective-permute-start.7 = (f32[2,128,512]{2,1,0:T(8,128)S(1)}, f32[2,128,512]{2,1,0:T(8,128)S(1)}, u32[]{:S(2)}, u32[]{:S(2)}) collective-permute-start(f32[2,128,512]{2,1,0:T(8,128)S(1)} %get-tuple-element.50), channel_id=1, source_target_pairs={{8,16},{16,8},{24,32},{32,24},{40,48},{48,40},{56,64},{64,56},{72,... | collective-permute-start | bytes 1572872 | tf_op jit(solution)/shard_map/ppermute | solution.py:362
  20.6 4.4 %collective-permute-start.5 = (f32[2,128,512]{2,1,0:T(8,128)S(1)}, f32[2,128,512]{2,1,0:T(8,128)S(1)}, u32[]{:S(2)}, u32[]{:S(2)}) collective-permute-start(f32[2,128,512]{2,1,0:T(8,128)S(1)} %get-tuple-element.48), channel_id=1, source_target_pairs={{8,16},{16,8},{24,32},{32,24},{40,48},{48,40},{56,64},{64,56},{72,... | collective-permute-start | bytes 1572872 | tf_op jit(solution)/shard_map/ppermute | solution.py:362
  25.0 3.3 %shard_map.75 = (f32[3,2,256,256]{3,2,1,0:T(8,128)S(1)}, f32[3,256,256]{2,1,0:T(8,128)S(1)}) custom-call(s32[8]{0:T(128)S(1)} %pad_add_fusion.offs, f32[2,256,256]{2,1,0:T(8,128)S(1)} %copy-done.2, f32[3,256,256]{2,1,0:T(8,128)S(1)} %bitcast.4), custom_call_target="tpu_custom_call" | custom-call | flops 3000000000 | bytes 1000000 | tf_op jit(solution)/shard_map/pallas_call | solution.py:384
  29.0 2.5 %shard_map.76.wave = f32[3,2,256,256]{3,2,1,0:T(8,128)S(1)} custom-call(s32[8]{0:T(128)S(1)} %pad_add_fusion.offs, f32[2,256,512]{2,1,0:T(8,128)S(1)} %get-tuple-element.45.wide, f32[2,128,512]{2,1,0:T(8,128)S(1)} %collective-permute-done.6.row_a, f32[2,128,512]{2,1,0:T(8,128)S(1)} %collective-permute-done.7.row_b, ...), custom_call_target="tpu_custom_call" | custom-call | flops 3000000000 | bytes 1000000 | tf_op jit(solution)/shard_map/pallas_call | solution.py:401
  31.6 3.0 %collective-permute-done.5.row_b = f32[2,128,512]{2,1,0:T(8,128)S(1)} collective-permute-done((f32[2,128,512]{2,1,0:T(8,128)S(1)}, f32[2,128,512]{2,1,0:T(8,128)S(1)}, u32[]{:S(2)}, u32[]{:S(2)}) %collective-permute-start.5) | collective-permute-done | bytes 524320 | tf_op jit(solution)/shard_map/ppermute | solution.py:362
  34.7 4.8 %shard_map.77 = (f32[2,256,512]{2,1,0:T(8,128)S(1)}, f32[2,128,512]{2,1,0:T(8,128)S(1)}, f32[2,128,512]{2,1,0:T(8,128)S(1)}, f32[3,2,256,256]{3,2,1,0:T(8,128)S(1)}) custom-call(s32[8]{0:T(128)S(1)} %pad_add_fusion.offs, f32[2,256,512]{2,1,0:T(8,128)S(1)} %get-tuple-element.46.wide, f32[2,128,512]{2,1,0:T(8,128)S(1)} %collective-permute-done.4.row_a, ...), custom_call_target="tpu_custom_call" | custom-call | flops 6000000000 | bytes 1000000 | tf_op jit(solution)/shard_map/pallas_call | solution.py:404
  39.4 2.9 %shard_map.78 = (f32[2,256,512]{2,1,0:T(8,128)S(1)}, f32[2,128,512]{2,1,0:T(8,128)S(1)}, f32[2,128,512]{2,1,0:T(8,128)S(1)}) custom-call(s32[8]{0:T(128)S(1)} %pad_add_fusion.offs, f32[3,2,256,256]{3,2,1,0:T(8,128)S(1)} %get-tuple-element.53.back, f32[3,2,256,256]{3,2,1,0:T(8,128)S(1)} %get-tuple-element.51.rolled, bf16[8,256,256]{2,1,0:T(8,128)(2,1)S(1)} %copy-done.3), custom_call_target="tpu_custom_call" | custom-call | flops 4000000000 | bytes 1000000 | tf_op jit(solution)/shard_map/pallas_call | solution.py:408
  42.5 3.0 %collective-permute-start.9 = (f32[2,128,512]{2,1,0:T(8,128)S(1)}, f32[2,128,512]{2,1,0:T(8,128)S(1)}, u32[]{:S(2)}, u32[]{:S(2)}) collective-permute-start(f32[2,128,512]{2,1,0:T(8,128)S(1)} %get-tuple-element.56), channel_id=1, source_target_pairs={{8,16},{16,8},{24,32},{32,24},{40,48},{48,40},{56,64},{64,56},{72,... | collective-permute-start | bytes 1572872 | tf_op jit(solution)/shard_map/ppermute | solution.py:362
  45.5 2.4 %collective-permute-start.13 = (f32[2,128,512]{2,1,0:T(8,128)S(1)}, f32[2,128,512]{2,1,0:T(8,128)S(1)}, u32[]{:S(2)}, u32[]{:S(2)}) collective-permute-start(f32[2,128,512]{2,1,0:T(8,128)S(1)} %get-tuple-element.63), channel_id=1, source_target_pairs={{8,16},{16,8},{24,32},{32,24},{40,48},{48,40},{56,64},{64,56},{72,... | collective-permute-start | bytes 1572872 | tf_op jit(solution)/shard_map/ppermute | solution.py:362
  47.9 6.9 %collective-permute-done.9.row_b = f32[2,128,512]{2,1,0:T(8,128)S(1)} collective-permute-done((f32[2,128,512]{2,1,0:T(8,128)S(1)}, f32[2,128,512]{2,1,0:T(8,128)S(1)}, u32[]{:S(2)}, u32[]{:S(2)}) %collective-permute-start.9) | collective-permute-done | bytes 524320 | tf_op jit(solution)/shard_map/ppermute | solution.py:362
  55.6 4.1 %collective-permute-start.11 = (f32[2,256,256]{2,1,0:T(8,128)S(1)}, f32[2,256,256]{2,1,0:T(8,128)S(1)}, u32[]{:S(2)}, u32[]{:S(2)}) collective-permute-start(f32[2,256,256]{2,1,0:T(8,128)S(1)} %get-tuple-element.59), channel_id=1, source_target_pairs={{0,7},{1,0},{2,1},{3,2},{4,3},{5,4},{6,5},{7,6},{8,15},{9,8},{10,9... | collective-permute-start | bytes 1572872 | tf_op jit(solution)/shard_map/ppermute | solution.py:353
  61.2 5.6 %collective-permute-start.15 = (f32[2,256,256]{2,1,0:T(8,128)S(1)}, f32[2,256,256]{2,1,0:T(8,128)S(1)}, u32[]{:S(2)}, u32[]{:S(2)}) collective-permute-start(f32[2,256,256]{2,1,0:T(8,128)S(1)} %get-tuple-element.66), channel_id=1, source_target_pairs={{0,7},{1,0},{2,1},{3,2},{4,3},{5,4},{6,5},{7,6},{8,15},{9,8},{10,9... | collective-permute-start | bytes 1572872 | tf_op jit(solution)/shard_map/ppermute | solution.py:353
  66.8 10.8 %collective-permute-done.10.from_left = f32[2,256,256]{2,1,0:T(8,128)S(1)} collective-permute-done((f32[2,256,256]{2,1,0:T(8,128)S(1)}, f32[2,256,256]{2,1,0:T(8,128)S(1)}, u32[]{:S(2)}, u32[]{:S(2)}) %collective-permute-start.10) | collective-permute-done | bytes 524320 | tf_op jit(solution)/shard_map/ppermute | solution.py:353
  77.6 0.8 shard_map.80
  78.6 5.8 %collective-permute-done.14.from_left = f32[2,256,256]{2,1,0:T(8,128)S(1)} collective-permute-done((f32[2,256,256]{2,1,0:T(8,128)S(1)}, f32[2,256,256]{2,1,0:T(8,128)S(1)}, u32[]{:S(2)}, u32[]{:S(2)}) %collective-permute-start.14) | collective-permute-done | bytes 524320 | tf_op jit(solution)/shard_map/ppermute | solution.py:353
  85.8 5.0 %collective-permute-done.19.row_b = f32[2,128,512]{2,1,0:T(8,128)S(1)} collective-permute-done((f32[2,128,512]{2,1,0:T(8,128)S(1)}, f32[2,128,512]{2,1,0:T(8,128)S(1)}, u32[]{:S(2)}, u32[]{:S(2)}) %collective-permute-start.19) | collective-permute-done | bytes 524320 | tf_op jit(solution)/shard_map/ppermute | solution.py:362
  90.8 2.5 %shard_map.83.wave = f32[3,2,256,256]{3,2,1,0:T(8,128)S(1)} custom-call(s32[8]{0:T(128)S(1)} %pad_add_fusion.offs, f32[2,256,512]{2,1,0:T(8,128)S(1)} %get-tuple-element.60.wide, f32[2,128,512]{2,1,0:T(8,128)S(1)} %collective-permute-done.18.row_a, f32[2,128,512]{2,1,0:T(8,128)S(1)} %collective-permute-done.19.row_b, ...), custom_call_target="tpu_custom_call" | custom-call | flops 3000000000 | bytes 1000000 | tf_op jit(solution)/shard_map/pallas_call | solution.py:401
  93.4 4.2 %collective-permute-done.17.row_b = f32[2,128,512]{2,1,0:T(8,128)S(1)} collective-permute-done((f32[2,128,512]{2,1,0:T(8,128)S(1)}, f32[2,128,512]{2,1,0:T(8,128)S(1)}, u32[]{:S(2)}, u32[]{:S(2)}) %collective-permute-start.17) | collective-permute-done | bytes 524320 | tf_op jit(solution)/shard_map/ppermute | solution.py:362
  97.5 4.8 %shard_map.84 = (f32[2,256,512]{2,1,0:T(8,128)S(1)}, f32[2,128,512]{2,1,0:T(8,128)S(1)}, f32[2,128,512]{2,1,0:T(8,128)S(1)}, f32[3,2,256,256]{3,2,1,0:T(8,128)S(1)}) custom-call(s32[8]{0:T(128)S(1)} %pad_add_fusion.offs, f32[2,256,512]{2,1,0:T(8,128)S(1)} %get-tuple-element.67.wide, f32[2,128,512]{2,1,0:T(8,128)S(1)} %collective-permute-done.16.row_a, ...), custom_call_target="tpu_custom_call" | custom-call | flops 6000000000 | bytes 1000000 | tf_op jit(solution)/shard_map/pallas_call | solution.py:404
  103.0 2.9 %shard_map.85 = (f32[2,256,512]{2,1,0:T(8,128)S(1)}, f32[2,128,512]{2,1,0:T(8,128)S(1)}, f32[2,128,512]{2,1,0:T(8,128)S(1)}) custom-call(s32[8]{0:T(128)S(1)} %pad_add_fusion.offs, f32[3,2,256,256]{3,2,1,0:T(8,128)S(1)} %get-tuple-element.72.back, f32[3,2,256,256]{3,2,1,0:T(8,128)S(1)} %get-tuple-element.51.rolled, bf16[8,256,256]{2,1,0:T(8,128)(2,1)S(1)} %copy-done.3), custom_call_target="tpu_custom_call" | custom-call | flops 4000000000 | bytes 1000000 | tf_op jit(solution)/shard_map/pallas_call | solution.py:408
  106.0 5.0 %collective-permute-start.21 = (f32[2,128,512]{2,1,0:T(8,128)S(1)}, f32[2,128,512]{2,1,0:T(8,128)S(1)}, u32[]{:S(2)}, u32[]{:S(2)}) collective-permute-start(f32[2,128,512]{2,1,0:T(8,128)S(1)} %get-tuple-element.75), channel_id=1, source_target_pairs={{8,16},{16,8},{24,32},{32,24},{40,48},{48,40},{56,64},{64,56},{72,... | collective-permute-start | bytes 1572872 | tf_op jit(solution)/shard_map/ppermute | solution.py:362
  110.9 3.8 %collective-permute-done.25.row_b = f32[2,128,512]{2,1,0:T(8,128)S(1)} collective-permute-done((f32[2,128,512]{2,1,0:T(8,128)S(1)}, f32[2,128,512]{2,1,0:T(8,128)S(1)}, u32[]{:S(2)}, u32[]{:S(2)}) %collective-permute-start.25) | collective-permute-done | bytes 524320 | tf_op jit(solution)/shard_map/ppermute | solution.py:362
  115.5 4.1 %collective-permute-start.27 = (f32[2,256,128]{2,1,0:T(8,128)S(1)}, f32[2,256,128]{2,1,0:T(8,128)S(1)}, u32[]{:S(2)}, u32[]{:S(2)}) collective-permute-start(f32[2,256,128]{2,1,0:T(8,128)S(1)} %get-tuple-element.84), channel_id=1, source_target_pairs={{0,7},{1,0},{2,1},{3,2},{4,3},{5,4},{6,5},{7,6},{8,15},{9,8},{10,9... | collective-permute-start | bytes 786440 | tf_op jit(solution)/shard_map/ppermute | solution.py:353
  119.6 2.7 %collective-permute-done.21.row_b = f32[2,128,512]{2,1,0:T(8,128)S(1)} collective-permute-done((f32[2,128,512]{2,1,0:T(8,128)S(1)}, f32[2,128,512]{2,1,0:T(8,128)S(1)}, u32[]{:S(2)}, u32[]{:S(2)}) %collective-permute-start.21) | collective-permute-done | bytes 524320 | tf_op jit(solution)/shard_map/ppermute | solution.py:362
  123.1 4.1 %collective-permute-start.23 = (f32[2,256,128]{2,1,0:T(8,128)S(1)}, f32[2,256,128]{2,1,0:T(8,128)S(1)}, u32[]{:S(2)}, u32[]{:S(2)}) collective-permute-start(f32[2,256,128]{2,1,0:T(8,128)S(1)} %get-tuple-element.78), channel_id=1, source_target_pairs={{0,7},{1,0},{2,1},{3,2},{4,3},{5,4},{6,5},{7,6},{8,15},{9,8},{10,9... | collective-permute-start | bytes 786440 | tf_op jit(solution)/shard_map/ppermute | solution.py:353
  127.3 4.2 %collective-permute-done.22.from_left = f32[2,256,128]{2,1,0:T(8,128)S(1)} collective-permute-done((f32[2,256,128]{2,1,0:T(8,128)S(1)}, f32[2,256,128]{2,1,0:T(8,128)S(1)}, u32[]{:S(2)}, u32[]{:S(2)}) %collective-permute-start.22) | collective-permute-done | bytes 262176 | tf_op jit(solution)/shard_map/ppermute | solution.py:353
  131.6 1.1 shard_map.89
  (57 shorter events, 8.9 us)
Async XLA Ops:
  0.0 13.7 %copy-start = (f32[4,256,256]{2,1,0:T(8,128)S(1)}, f32[4,256,256]{2,1,0:T(8,128)}, u32[]{:S(2)}) copy-start(f32[4,256,256]{2,1,0:T(8,128)} %own.3) | copy-start | bytes 3145732
  0.0 11.4 %copy-start.5 = (s32[1,1,3,2]{2,3,1,0:T(2,128)S(1)}, s32[1,1,3,2]{2,3,1,0:T(2,128)}, u32[]{:S(2)}) copy-start(s32[1,1,3,2]{2,3,1,0:T(2,128)} %param.9) | copy-start | bytes 76
  1.4 12.3 %collective-permute-start.1 = (f32[2,256,128]{2,1,0:T(8,128)S(1)}, f32[2,256,128]{2,1,0:T(8,128)S(1)}, u32[]{:S(2)}, u32[]{:S(2)}) collective-permute-start(f32[2,256,128]{2,1,0:T(8,128)S(1)} %get-tuple-element.87), channel_id=1, source_target_pairs={{0,1},{1,2},{2,3},{3,4},{4,5},{5,6},{6,7},{7,0},{8,9},{9,10},{10,1... | collective-permute-start | bytes 786440 | tf_op jit(solution)/shard_map/ppermute | solution.py:353
  3.5 10.2 %collective-permute-start = (f32[2,256,128]{2,1,0:T(8,128)S(1)}, f32[2,256,128]{2,1,0:T(8,128)S(1)}, u32[]{:S(2)}, u32[]{:S(2)}) collective-permute-start(f32[2,256,128]{2,1,0:T(8,128)S(1)} %get-tuple-element.88), channel_id=1, source_target_pairs={{0,7},{1,0},{2,1},{3,2},{4,3},{5,4},{6,5},{7,6},{8,15},{9,8},{10,9... | collective-permute-start | bytes 786440 | tf_op jit(solution)/shard_map/ppermute | solution.py:353
  6.6 13.2 %collective-permute-start.3 = (f32[2,256,128]{2,1,0:T(8,128)S(1)}, f32[2,256,128]{2,1,0:T(8,128)S(1)}, u32[]{:S(2)}, u32[]{:S(2)}) collective-permute-start(f32[2,256,128]{2,1,0:T(8,128)S(1)} %get-tuple-element.85), channel_id=1, source_target_pairs={{0,1},{1,2},{2,3},{3,4},{4,5},{5,6},{6,7},{7,0},{8,9},{9,10},{10,1... | collective-permute-start | bytes 786440 | tf_op jit(solution)/shard_map/ppermute | solution.py:353
  6.6 13.2 %collective-permute-start.2 = (f32[2,256,128]{2,1,0:T(8,128)S(1)}, f32[2,256,128]{2,1,0:T(8,128)S(1)}, u32[]{:S(2)}, u32[]{:S(2)}) collective-permute-start(f32[2,256,128]{2,1,0:T(8,128)S(1)} %get-tuple-element.86), channel_id=1, source_target_pairs={{0,7},{1,0},{2,1},{3,2},{4,3},{5,4},{6,5},{7,6},{8,15},{9,8},{10,9... | collective-permute-start | bytes 786440 | tf_op jit(solution)/shard_map/ppermute | solution.py:353
  11.7 13.3 %copy-start.1 = (f32[1,1,3,256,256]{4,3,2,1,0:T(8,128)S(1)}, f32[1,1,3,256,256]{4,3,2,1,0:T(8,128)}, u32[]{:S(2)}) copy-start(f32[1,1,3,256,256]{4,3,2,1,0:T(8,128)} %param.11) | copy-start | bytes 2359300
  11.7 13.3 %copy-start.2 = (f32[2,256,256]{2,1,0:T(8,128)S(1)}, f32[2,256,256]{2,1,0:T(8,128)}, u32[]{:S(2)}) copy-start(f32[2,256,256]{2,1,0:T(8,128)} %probe.1) | copy-start | bytes 1572868
  14.4 14.0 %collective-permute-start.6 = (f32[2,128,512]{2,1,0:T(8,128)S(1)}, f32[2,128,512]{2,1,0:T(8,128)S(1)}, u32[]{:S(2)}, u32[]{:S(2)}) collective-permute-start(f32[2,128,512]{2,1,0:T(8,128)S(1)} %get-tuple-element.49), channel_id=1, source_target_pairs={{0,8},{8,0},{16,24},{24,16},{32,40},{40,32},{48,56},{56,48},{64,72... | collective-permute-start | bytes 1572872 | tf_op jit(solution)/shard_map/ppermute | solution.py:362
  14.5 14.5 %collective-permute-start.7 = (f32[2,128,512]{2,1,0:T(8,128)S(1)}, f32[2,128,512]{2,1,0:T(8,128)S(1)}, u32[]{:S(2)}, u32[]{:S(2)}) collective-permute-start(f32[2,128,512]{2,1,0:T(8,128)S(1)} %get-tuple-element.50), channel_id=1, source_target_pairs={{8,16},{16,8},{24,32},{32,24},{40,48},{48,40},{56,64},{64,56},{72,... | collective-permute-start | bytes 1572872 | tf_op jit(solution)/shard_map/ppermute | solution.py:362
  20.5 11.1 %collective-permute-start.4 = (f32[2,128,512]{2,1,0:T(8,128)S(1)}, f32[2,128,512]{2,1,0:T(8,128)S(1)}, u32[]{:S(2)}, u32[]{:S(2)}) collective-permute-start(f32[2,128,512]{2,1,0:T(8,128)S(1)} %get-tuple-element.47), channel_id=1, source_target_pairs={{0,8},{8,0},{16,24},{24,16},{32,40},{40,32},{48,56},{56,48},{64,72... | collective-permute-start | bytes 1572872 | tf_op jit(solution)/shard_map/ppermute | solution.py:362
  20.6 14.1 %collective-permute-start.5 = (f32[2,128,512]{2,1,0:T(8,128)S(1)}, f32[2,128,512]{2,1,0:T(8,128)S(1)}, u32[]{:S(2)}, u32[]{:S(2)}) collective-permute-start(f32[2,128,512]{2,1,0:T(8,128)S(1)} %get-tuple-element.48), channel_id=1, source_target_pairs={{8,16},{16,8},{24,32},{32,24},{40,48},{48,40},{56,64},{64,56},{72,... | collective-permute-start | bytes 1572872 | tf_op jit(solution)/shard_map/ppermute | solution.py:362
  42.4 5.5 %collective-permute-start.8 = (f32[2,128,512]{2,1,0:T(8,128)S(1)}, f32[2,128,512]{2,1,0:T(8,128)S(1)}, u32[]{:S(2)}, u32[]{:S(2)}) collective-permute-start(f32[2,128,512]{2,1,0:T(8,128)S(1)} %get-tuple-element.55), channel_id=1, source_target_pairs={{0,8},{8,0},{16,24},{24,16},{32,40},{40,32},{48,56},{56,48},{64,72... | collective-permute-start | bytes 1572872 | tf_op jit(solution)/shard_map/ppermute | solution.py:362
  42.5 12.3 %collective-permute-start.9 = (f32[2,128,512]{2,1,0:T(8,128)S(1)}, f32[2,128,512]{2,1,0:T(8,128)S(1)}, u32[]{:S(2)}, u32[]{:S(2)}) collective-permute-start(f32[2,128,512]{2,1,0:T(8,128)S(1)} %get-tuple-element.56), channel_id=1, source_target_pairs={{8,16},{16,8},{24,32},{32,24},{40,48},{48,40},{56,64},{64,56},{72,... | collective-permute-start | bytes 1572872 | tf_op jit(solution)/shard_map/ppermute | solution.py:362
  45.5 14.2 %collective-permute-start.12 = (f32[2,128,512]{2,1,0:T(8,128)S(1)}, f32[2,128,512]{2,1,0:T(8,128)S(1)}, u32[]{:S(2)}, u32[]{:S(2)}) collective-permute-start(f32[2,128,512]{2,1,0:T(8,128)S(1)} %get-tuple-element.62), channel_id=1, source_target_pairs={{0,8},{8,0},{16,24},{24,16},{32,40},{40,32},{48,56},{56,48},{64,72... | collective-permute-start | bytes 1572872 | tf_op jit(solution)/shard_map/ppermute | solution.py:362
  45.5 14.9 %collective-permute-start.13 = (f32[2,128,512]{2,1,0:T(8,128)S(1)}, f32[2,128,512]{2,1,0:T(8,128)S(1)}, u32[]{:S(2)}, u32[]{:S(2)}) collective-permute-start(f32[2,128,512]{2,1,0:T(8,128)S(1)} %get-tuple-element.63), channel_id=1, source_target_pairs={{8,16},{16,8},{24,32},{32,24},{40,48},{48,40},{56,64},{64,56},{72,... | collective-permute-start | bytes 1572872 | tf_op jit(solution)/shard_map/ppermute | solution.py:362
  55.5 22.1 %collective-permute-start.10 = (f32[2,256,256]{2,1,0:T(8,128)S(1)}, f32[2,256,256]{2,1,0:T(8,128)S(1)}, u32[]{:S(2)}, u32[]{:S(2)}) collective-permute-start(f32[2,256,256]{2,1,0:T(8,128)S(1)} %get-tuple-element.58), channel_id=1, source_target_pairs={{0,1},{1,2},{2,3},{3,4},{4,5},{5,6},{6,7},{7,0},{8,9},{9,10},{10,1... | collective-permute-start | bytes 1572872 | tf_op jit(solution)/shard_map/ppermute | solution.py:353
  55.6 22.1 %collective-permute-start.11 = (f32[2,256,256]{2,1,0:T(8,128)S(1)}, f32[2,256,256]{2,1,0:T(8,128)S(1)}, u32[]{:S(2)}, u32[]{:S(2)}) collective-permute-start(f32[2,256,256]{2,1,0:T(8,128)S(1)} %get-tuple-element.59), channel_id=1, source_target_pairs={{0,7},{1,0},{2,1},{3,2},{4,3},{5,4},{6,5},{7,6},{8,15},{9,8},{10,9... | collective-permute-start | bytes 1572872 | tf_op jit(solution)/shard_map/ppermute | solution.py:353
  61.1 23.2 %collective-permute-start.14 = (f32[2,256,256]{2,1,0:T(8,128)S(1)}, f32[2,256,256]{2,1,0:T(8,128)S(1)}, u32[]{:S(2)}, u32[]{:S(2)}) collective-permute-start(f32[2,256,256]{2,1,0:T(8,128)S(1)} %get-tuple-element.65), channel_id=1, source_target_pairs={{0,1},{1,2},{2,3},{3,4},{4,5},{5,6},{6,7},{7,0},{8,9},{9,10},{10,1... | collective-permute-start | bytes 1572872 | tf_op jit(solution)/shard_map/ppermute | solution.py:353
  61.2 23.2 %collective-permute-start.15 = (f32[2,256,256]{2,1,0:T(8,128)S(1)}, f32[2,256,256]{2,1,0:T(8,128)S(1)}, u32[]{:S(2)}, u32[]{:S(2)}) collective-permute-start(f32[2,256,256]{2,1,0:T(8,128)S(1)} %get-tuple-element.66), channel_id=1, source_target_pairs={{0,7},{1,0},{2,1},{3,2},{4,3},{5,4},{6,5},{7,6},{8,15},{9,8},{10,9... | collective-permute-start | bytes 1572872 | tf_op jit(solution)/shard_map/ppermute | solution.py:353
  78.4 7.4 %collective-permute-start.18 = (f32[2,128,512]{2,1,0:T(8,128)S(1)}, f32[2,128,512]{2,1,0:T(8,128)S(1)}, u32[]{:S(2)}, u32[]{:S(2)}) collective-permute-start(f32[2,128,512]{2,1,0:T(8,128)S(1)} %get-tuple-element.70), channel_id=1, source_target_pairs={{0,8},{8,0},{16,24},{24,16},{32,40},{40,32},{48,56},{56,48},{64,72... | collective-permute-start | bytes 1572872 | tf_op jit(solution)/shard_map/ppermute | solution.py:362
  78.5 12.3 %collective-permute-start.19 = (f32[2,128,512]{2,1,0:T(8,128)S(1)}, f32[2,128,512]{2,1,0:T(8,128)S(1)}, u32[]{:S(2)}, u32[]{:S(2)}) collective-permute-start(f32[2,128,512]{2,1,0:T(8,128)S(1)} %get-tuple-element.71), channel_id=1, source_target_pairs={{8,16},{16,8},{24,32},{32,24},{40,48},{48,40},{56,64},{64,56},{72,... | collective-permute-start | bytes 1572872 | tf_op jit(solution)/shard_map/ppermute | solution.py:362
  85.1 8.2 %collective-permute-start.16 = (f32[2,128,512]{2,1,0:T(8,128)S(1)}, f32[2,128,512]{2,1,0:T(8,128)S(1)}, u32[]{:S(2)}, u32[]{:S(2)}) collective-permute-start(f32[2,128,512]{2,1,0:T(8,128)S(1)} %get-tuple-element.68), channel_id=1, source_target_pairs={{0,8},{8,0},{16,24},{24,16},{32,40},{40,32},{48,56},{56,48},{64,72... | collective-permute-start | bytes 1572872 | tf_op jit(solution)/shard_map/ppermute | solution.py:362
  85.2 12.3 %collective-permute-start.17 = (f32[2,128,512]{2,1,0:T(8,128)S(1)}, f32[2,128,512]{2,1,0:T(8,128)S(1)}, u32[]{:S(2)}, u32[]{:S(2)}) collective-permute-start(f32[2,128,512]{2,1,0:T(8,128)S(1)} %get-tuple-element.69), channel_id=1, source_target_pairs={{8,16},{16,8},{24,32},{32,24},{40,48},{48,40},{56,64},{64,56},{72,... | collective-permute-start | bytes 1572872 | tf_op jit(solution)/shard_map/ppermute | solution.py:362
  102.3 8.6 %collective-permute-start.24 = (f32[2,128,512]{2,1,0:T(8,128)S(1)}, f32[2,128,512]{2,1,0:T(8,128)S(1)}, u32[]{:S(2)}, u32[]{:S(2)}) collective-permute-start(f32[2,128,512]{2,1,0:T(8,128)S(1)} %get-tuple-element.80), channel_id=1, source_target_pairs={{0,8},{8,0},{16,24},{24,16},{32,40},{40,32},{48,56},{56,48},{64,72... | collective-permute-start | bytes 1572872 | tf_op jit(solution)/shard_map/ppermute | solution.py:362
  102.4 12.3 %collective-permute-start.25 = (f32[2,128,512]{2,1,0:T(8,128)S(1)}, f32[2,128,512]{2,1,0:T(8,128)S(1)}, u32[]{:S(2)}, u32[]{:S(2)}) collective-permute-start(f32[2,128,512]{2,1,0:T(8,128)S(1)} %get-tuple-element.81), channel_id=1, source_target_pairs={{8,16},{16,8},{24,32},{32,24},{40,48},{48,40},{56,64},{64,56},{72,... | collective-permute-start | bytes 1572872 | tf_op jit(solution)/shard_map/ppermute | solution.py:362
  105.9 13.7 %collective-permute-start.20 = (f32[2,128,512]{2,1,0:T(8,128)S(1)}, f32[2,128,512]{2,1,0:T(8,128)S(1)}, u32[]{:S(2)}, u32[]{:S(2)}) collective-permute-start(f32[2,128,512]{2,1,0:T(8,128)S(1)} %get-tuple-element.74), channel_id=1, source_target_pairs={{0,8},{8,0},{16,24},{24,16},{32,40},{40,32},{48,56},{56,48},{64,72... | collective-permute-start | bytes 1572872 | tf_op jit(solution)/shard_map/ppermute | solution.py:362
  106.0 16.3 %collective-permute-start.21 = (f32[2,128,512]{2,1,0:T(8,128)S(1)}, f32[2,128,512]{2,1,0:T(8,128)S(1)}, u32[]{:S(2)}, u32[]{:S(2)}) collective-permute-start(f32[2,128,512]{2,1,0:T(8,128)S(1)} %get-tuple-element.75), channel_id=1, source_target_pairs={{8,16},{16,8},{24,32},{32,24},{40,48},{48,40},{56,64},{64,56},{72,... | collective-permute-start | bytes 1572872 | tf_op jit(solution)/shard_map/ppermute | solution.py:362
  115.4 11.8 %collective-permute-start.26 = (f32[2,256,128]{2,1,0:T(8,128)S(1)}, f32[2,256,128]{2,1,0:T(8,128)S(1)}, u32[]{:S(2)}, u32[]{:S(2)}) collective-permute-start(f32[2,256,128]{2,1,0:T(8,128)S(1)} %get-tuple-element.83), channel_id=1, source_target_pairs={{0,1},{1,2},{2,3},{3,4},{4,5},{5,6},{6,7},{7,0},{8,9},{9,10},{10,1... | collective-permute-start | bytes 786440 | tf_op jit(solution)/shard_map/ppermute | solution.py:353
  115.5 11.7 %collective-permute-start.27 = (f32[2,256,128]{2,1,0:T(8,128)S(1)}, f32[2,256,128]{2,1,0:T(8,128)S(1)}, u32[]{:S(2)}, u32[]{:S(2)}) collective-permute-start(f32[2,256,128]{2,1,0:T(8,128)S(1)} %get-tuple-element.84), channel_id=1, source_target_pairs={{0,7},{1,0},{2,1},{3,2},{4,3},{5,4},{6,5},{7,6},{8,15},{9,8},{10,9... | collective-permute-start | bytes 786440 | tf_op jit(solution)/shard_map/ppermute | solution.py:353
  123.0 8.6 %collective-permute-start.22 = (f32[2,256,128]{2,1,0:T(8,128)S(1)}, f32[2,256,128]{2,1,0:T(8,128)S(1)}, u32[]{:S(2)}, u32[]{:S(2)}) collective-permute-start(f32[2,256,128]{2,1,0:T(8,128)S(1)} %get-tuple-element.77), channel_id=1, source_target_pairs={{0,1},{1,2},{2,3},{3,4},{4,5},{5,6},{6,7},{7,0},{8,9},{9,10},{10,1... | collective-permute-start | bytes 786440 | tf_op jit(solution)/shard_map/ppermute | solution.py:353
  123.1 8.5 %collective-permute-start.23 = (f32[2,256,128]{2,1,0:T(8,128)S(1)}, f32[2,256,128]{2,1,0:T(8,128)S(1)}, u32[]{:S(2)}, u32[]{:S(2)}) collective-permute-start(f32[2,256,128]{2,1,0:T(8,128)S(1)} %get-tuple-element.78), channel_id=1, source_target_pairs={{0,7},{1,0},{2,1},{3,2},{4,3},{5,4},{6,5},{7,6},{8,15},{9,8},{10,9... | collective-permute-start | bytes 786440 | tf_op jit(solution)/shard_map/ppermute | solution.py:353
  (2 other events, 9.6 us)
